TPU v7x, 32 devices: a whole 2x2x4 slice. The times are simulated.
32 devices in a mesh: gx: 2 (over x), gy: 4 (over y, core), gz: 4 (over z).
Axes of the slice: x: 2, y: 2, z: 4, core: 2. Of those that a mesh axis runs over, the one named last changes fastest.
Arguments:
- rhs: float32 [8, 8, 2, 16, 512], P(None, None, 'gx', 'gy', 'gz'), as said below
- blocks: bfloat16 [7, 8, 8, 2, 16, 512], P(None, None, None, 'gx', 'gy', 'gz'), as said below
Outputs:
- basis: float32 [4, 8, 8, 2, 16, 512], P(None, None, None, 'gx', 'gy', 'gz')
- hess: float32 [4, 8, 3, 8], replicated
Inputs may be any that keep to these rules, and one draw needn't show every extreme that they name: `rhs`: each cell's value is a random draw times a positive scale that varies smoothly over the grid. The operator couples each cell only to itself and its six face neighbours; its blocks are full and the block Krylov spaces keep full rank.
All inputs are finite; a program needn't handle non-finite values.
Results may differ from a plain program's by a relative error of at most 0.001.
Values sent between devices are 32-bit elements; how exact they have to be, the bound alone decides.
A program may use at most 64 MiB of HBM per device.

v0:
```python
import functools

import jax
import jax.numpy as jnp
from jax import lax
from jax.experimental import pallas as pl
from jax.experimental.pallas import tpu as pltpu
from jax.sharding import PartitionSpec as P

ITERS = 3
F32 = jnp.float32
HIGH = lax.Precision.HIGHEST
AXES = ("gx", "gy", "gz")


def dot_nt(a, b):
    return lax.dot_general(a, b, (((1,), (1,)), ((), ())), precision=HIGH, preferred_element_type=F32)


def dot_nn(a, b):
    return lax.dot_general(a, b, (((1,), (0,)), ((), ())), precision=HIGH, preferred_element_type=F32)


def kernel(
    mesh_sizes, nb, nr, ly, lz,
    rhs_hbm, blk_hbm, basis_hbm, hess_ref,
    rv, bv, vp, p1, p3, xb, zs, zr, ce, zp, ab, ob,
    x_send, x_recv, y_send, y_recv, z_send, z_recv, a_send, a_recv, in_sem, out_sem, known,
):
    nx, ny, nz = mesh_sizes
    ndev = nx * ny * nz
    gx, gy, gz = (lax.axis_index(a) for a in AXES)
    me = (gx * ny + gy) * nz + gz
    cells = ndev * ly * lz

    row = lax.broadcasted_iota(jnp.int32, (8, 128), 0)
    lane = lax.broadcasted_iota(jnp.int32, (8, 128), 1)

    def peer(d):
        t = lax.rem(me + d, ndev)
        return (t // (ny * nz), (t // nz) % ny, t % nz)

    barrier = pltpu.get_barrier_semaphore()

    def greet(sem, axis):
        size, at = {"gx": (nx, gx), "gy": (ny, gy), "gz": (nz, gz)}[axis]

        def body(d, c):
            pl.semaphore_signal(sem, inc=1, device_id={axis: lax.rem(at + d, size)},
                                device_id_type=pl.DeviceIdType.MESH)
            return c
        lax.fori_loop(1, size, body, 0)

    in_rhs = pltpu.make_async_copy(rhs_hbm, rv, in_sem.at[0])
    in_blk = pltpu.make_async_copy(blk_hbm, bv, in_sem.at[1])
    in_rhs.start()
    in_blk.start()
    for axis in AXES:
        greet(barrier, axis)

    if nx == 1:
        x_sides = []
    elif nx == 2:
        x_sides = [(1 + gx, None, 1 - gx)]
    else:
        x_sides = [(1, gx < nx - 1, gx + 1), (2, gx > 0, gx - 1)]

    def when(cond, fn):
        if cond is None:
            fn()
        else:
            pl.when(cond)(fn)

    def remote(src, dst, ssem, rsem, dev):
        return pltpu.make_async_remote_copy(
            src_ref=src, dst_ref=dst, send_sem=ssem, recv_sem=rsem,
            device_id=dev, device_id_type=pl.DeviceIdType.MESH,
        )

    def x_copy(n, side, y):
        opposite = side if nx == 2 else 1 - side
        return remote(vp.at[n, 1 + y], xb.at[n, opposite, y], x_send.at[n, side, y],
                      x_recv.at[n, opposite, y], {"gx": x_sides[side][2]})

    def x_arrived(n, side, y):
        remote(vp.at[n, 1 + y], xb.at[n, side, y], x_send.at[n, side, y],
               x_recv.at[n, side, y], {"gx": x_sides[side][2]}).wait_recv()

    def y_copy(n, side):
        if side == 0:
            return remote(vp.at[n, ly], vp.at[n, 0], y_send.at[n, 0], y_recv.at[n, 0], {"gy": gy + 1})
        return remote(vp.at[n, 1], vp.at[n, ly + 1], y_send.at[n, 1], y_recv.at[n, 1], {"gy": gy - 1})

    def z_copy(n, side, y):
        target = gz - 1 if side == 0 else gz + 1
        return remote(zs.at[n, side, y], zr.at[n, side, y], z_send.at[n, side, y],
                      z_recv.at[n, side, y], {"gz": target})

    y_to = (gy < ny - 1, gy > 0)
    y_from = (gy > 0, gy < ny - 1)
    z_to = (gz > 0, gz < nz - 1)
    z_from = (gz < nz - 1, gz > 0)

    for side in range(2):
        @pl.when(jnp.logical_not(y_from[side]))
        def _():
            for n in range(ITERS):
                vp[n, 0 if side == 0 else ly + 1] = jnp.zeros((nb * 8, 128), F32)

        @pl.when(jnp.logical_not(z_from[side]))
        def _():
            for n in range(ITERS):
                zr[n, side] = jnp.zeros((ly, 8, 128), F32)

    if nx > 2:
        for side in range(2):
            @pl.when(jnp.logical_not(x_sides[side][1]))
            def _():
                for n in range(ITERS):
                    xb[n, side] = jnp.zeros((ly, nb * 8, 128), F32)

    def send_row(n, y):
        for side, entry in enumerate(x_sides):
            when(entry[1], lambda: x_copy(n, side, y).start())
        first = jnp.zeros((8, 128), F32)
        last = jnp.zeros((8, 128), F32)
        for a in range(nb):
            v = vp[n, 1 + y, a * 8:(a + 1) * 8]
            first = jnp.where(lane == a, pltpu.roll(v, a, 1) if a else v, first)
            last = jnp.where(lane == a, pltpu.roll(v, a + 1, 1), last)
        zs[n, 0, y] = first
        zs[n, 1, y] = last
        for side in range(2):
            pl.when(z_to[side])(lambda: z_copy(n, side, y).start())
        if y == ly - 1:
            pl.when(y_to[0])(lambda: y_copy(n, 0).start())
        if y == 0:
            pl.when(y_to[1])(lambda: y_copy(n, 1).start())

    order = [0] + ([ly - 1] if ly > 1 else []) + list(range(1, ly - 1))

    in_rhs.wait()
    for y in order:
        for a in range(nb):
            vp[0, 1 + y, a * 8:(a + 1) * 8] = rv[pl.ds(a * nr * ly + y, 8, stride=ly), :]
    pl.semaphore_wait(barrier, nx + ny + nz - 3)
    greet(known.at[0], "gy")
    for y in order:
        send_row(0, y)
    pl.semaphore_wait(known.at[0], ny - 1)
    greet(known.at[1], "gx")

    in_blk.wait()
    terms = [0, 3, 4, 5, 6] + [e[0] for e in x_sides]
    total_abs = jnp.zeros((8, 128), F32)
    for t, k in enumerate(terms):
        def expand(i, carry):
            rows = bv[k, i].astype(F32)
            for j in range(nb):
                for y in range(ly):
                    r = j * ly + y
                    wide = jnp.broadcast_to(rows[r:r + 1], (8, 128))
                    ce[t, y, j, pl.ds(pl.multiple_of(i * 8, 8), 8), :] = wide
                    if j == 0 and y == 0:
                        pass
            return carry + jnp.sum(jnp.abs(rows), axis=0, keepdims=True)
        total_abs = lax.fori_loop(0, nb, expand, total_abs)
    trace = jnp.zeros((8, 128), F32)
    for y in range(ly):
        for i in range(nb):
            trace = trace + ce[0, y, i, i * 8:(i + 1) * 8]

    def wide(field):
        return jnp.concatenate(
            [field(y, a) for y in range(ly) for a in range(nb)], axis=1)

    def eight(a):
        return a * 8 if isinstance(a, int) else pl.multiple_of(a * 8, 8)

    def blockview(ref, n, off):
        if n is None:
            return lambda y, a: ref[y, pl.ds(eight(a), 8), :]
        return lambda y, a: ref[n, off + y, pl.ds(eight(a), 8), :]

    views = [blockview(vp, 0, 1), blockview(p1, None, 0), blockview(vp, 2, 1), blockview(p3, None, 0)]

    def stack(count):
        return jnp.concatenate([wide(v) for v in views[:count]], axis=0)

    def gram_row(n, y, acc):
        def body(a, acc):
            p = views[n](y, a)
            parts = []
            for i in range(n + 1):
                q = views[i](y, a)
                for d in range(8):
                    parts.append(acc[i * 8 + d] + p * (pltpu.roll(q, 8 - d, 0) if d else q))
            return tuple(parts)
        return lax.fori_loop(0, nb, body, acc)

    def gram_zero(n):
        return tuple(jnp.zeros((8, 128), F32) for _ in range(8 * (n + 1)))

    def gram_end(acc):
        d8 = jnp.zeros((8, 128), F32)
        for k, part in enumerate(acc):
            where = lane % 32 == (k // 8) * 8 + (row + k % 8) % 8
            d8 = jnp.where(where, jnp.sum(part, axis=1, keepdims=True), d8)
        return d8

    def gram(n):
        acc = gram_zero(n)
        for y in range(ly):
            acc = gram_row(n, y, acc)
        return gram_end(acc)

    def ar_start(m, d8):
        packed = jnp.where(lane // 32 == row % 4, d8, 0.0)
        ab[m, me, 0:1] = jnp.sum(packed[0:4], axis=0, keepdims=True)
        ab[m, me, 1:2] = jnp.sum(packed[4:8], axis=0, keepdims=True)

        def body(d, c):
            remote(ab.at[m, me], ab.at[m, me], a_send.at[m], a_recv.at[m], peer(d)).start()
            return c
        lax.fori_loop(1, ndev, body, 0)

    def ar_done(m):
        pltpu.make_async_copy(ab.at[m, 0:ndev - 1], ab.at[m, 0:ndev - 1], a_recv.at[m]).wait()
        total = jnp.sum(ab[m], axis=0)
        z = jnp.where(row < 4, total[0:1], total[1:2])
        z = jnp.where(lane // 32 == row % 4, z, 0.0)
        z = z + pltpu.roll(z, 64, 1)
        return z + pltpu.roll(z, 32, 1)

    lane_sum = lambda x: jnp.sum(x, axis=1, keepdims=True)
    d0 = gram(0)
    d0 = d0 + jnp.where(lane % 32 == 8, lane_sum(trace), 0.0)
    d0 = d0 + jnp.where(lane % 32 == 9, lane_sum(total_abs), 0.0)
    pl.semaphore_wait(known.at[1], nx - 1)
    ar_start(0, d0)

    def local_terms(n, y):
        pl_z = [z_from[0], z_from[1]]
        for side in range(2):
            pl.when(pl_z[side])(lambda: z_copy(n, side, y).wait_recv())
        if y == 0:
            pl.when(y_from[0])(lambda: y_copy(n, 0).wait_recv())
        if y == ly - 1:
            pl.when(y_from[1])(lambda: y_copy(n, 1).wait_recv())
        plus, minus = zr[n, 0, y], zr[n, 1, y]
        for j in range(nb):
            v = vp[n, 1 + y, j * 8:(j + 1) * 8]
            zp[0, j * 8:(j + 1) * 8] = jnp.where(
                lane == lz - 1, pltpu.roll(plus, lz - 1 - j, 1), pltpu.roll(v, lz - 1, 1))
            zp[1, j * 8:(j + 1) * 8] = jnp.where(
                lane == 0, pltpu.roll(minus, lz - j, 1) if j else minus, pltpu.roll(v, 1, 1))

        def body(j, acc):
            at = pl.ds(pl.multiple_of(j * 8, 8), 8)
            values = [vp[n, 1 + y, at, :], vp[n, 2 + y, at, :], vp[n, y, at, :], zp[0, at, :], zp[1, at, :]]
            for t, v in enumerate(values):
                acc = acc + ce[t, y, j].reshape(nb, 8, 128) * v[None]
            return acc
        return lax.fori_loop(0, nb, body, jnp.zeros((nb, 8, 128), F32))

    def x_terms(n, y, acc):
        for side, entry in enumerate(x_sides):
            when(entry[1], lambda: x_arrived(n, side, y))

            def body(j, acc):
                at = pl.ds(pl.multiple_of(j * 8, 8), 8)
                return acc + ce[5 + side, y, j].reshape(nb, 8, 128) * xb[n, side, y, at, :][None]
            acc = lax.fori_loop(0, nb, body, acc)
        return acc.reshape(nb * 8, 128)

    weights, factors = [], []
    empty = jnp.zeros((8, 128), F32)

    def pad_rows(pieces):
        return jnp.concatenate(pieces + [empty] * (16 - len(pieces)), axis=0)

    def factor(n, red):
        base = 8 * n
        unit = jnp.where(lane == base + row, 1.0, 0.0).astype(F32)
        d = jnp.where(lane < base + 8, red, 0.0)
        shifted = pltpu.roll(d, 128 - base, 1) if n else d
        if n:
            rt = dot_nt(d, pad_rows(weights))
            s = shifted - dot_nt(rt, pad_rows([rt]))
            aug = unit - rt
        else:
            rt = empty
            s = shifted
            aug = unit
        cols = [jnp.broadcast_to(s[:, c:c + 1], (8, 128)) for c in range(8)]
        low = rt
        for k in range(8):
            piv = jnp.broadcast_to(cols[k][k:k + 1], (8, 128))
            rs = lax.rsqrt(piv)
            rs = rs * (1.5 - 0.5 * piv * rs * rs)
            lk = jnp.where(row >= k, cols[k] * rs, 0.0)
            low = low + jnp.where(lane == base + k, lk, 0.0)
            arow = jnp.broadcast_to(aug[k:k + 1], (8, 128)) * rs
            aug = jnp.where(row == k, arow, aug - jnp.where(row > k, lk, 0.0) * arow)
            for c in range(k + 1, 8):
                cols[c] = cols[c] - lk * jnp.broadcast_to(lk[c:c + 1], (8, 128))
        weights.append(dot_nn(aug, pad_rows(weights + [unit])) if n else aug)
        factors.append(low)

    def emit(n):
        q = dot_nn(weights[n][:, :8 * (n + 1)], stack(n + 1))
        for y in range(ly):
            for a in range(nb):
                c = (y * nb + a) * 128
                ob[n, pl.ds(a * nr * ly + y, 8, stride=ly), :] = q[:, c:c + 128]
        pltpu.make_async_copy(ob.at[n], basis_hbm.at[n], out_sem.at[n]).start()

    for y in order:
        vp[1, 1 + y] = x_terms(0, y, local_terms(0, y))
        send_row(1, y)
    red0 = ar_done(0)
    sigma = jnp.broadcast_to(red0[0:1, 8:9] / (8.0 * cells), (8, 128))
    nu = jnp.broadcast_to(red0[0:1, 9:10] / (8.0 * cells), (8, 128))
    inv = 1.0 / nu
    sig1, inv1 = sigma[0:1], inv[0:1]
    for y in range(ly):
        p1[y] = (vp[1, 1 + y] - sig1 * vp[0, 1 + y]) * inv1
    ar_start(1, gram(1))

    acc = gram_zero(2)
    for y in order:
        image = x_terms(1, y, local_terms(1, y))
        vp[2, 1 + y] = ((image - sig1 * vp[1, 1 + y]) * inv1 - sig1 * p1[y]) * inv1
        send_row(2, y)
        acc = gram_row(2, y, acc)
    ar_start(2, gram_end(acc))

    acc = gram_zero(3)
    for y in order:
        image = x_terms(2, y, local_terms(2, y))
        p3[y] = (image - sig1 * vp[2, 1 + y]) * inv1
        acc = gram_row(3, y, acc)
    ar_start(3, gram_end(acc))
    factor(0, red0)
    emit(0)

    factor(1, ar_done(1))
    emit(1)
    factor(2, ar_done(2))
    emit(2)
    factor(3, ar_done(3))
    emit(3)
    h = dot_nn(jnp.concatenate(weights[:3] + [empty], axis=0), pad_rows(factors[1:]))
    hr = lax.broadcasted_iota(jnp.int32, (32, 128), 0)
    hl = lax.broadcasted_iota(jnp.int32, (32, 128), 1)
    hess_ref[...] = h * nu[0:1] + jnp.where(hr == hl, sigma[0:1], 0.0)

    for n in range(ITERS):
        for y in range(ly):
            for side, entry in enumerate(x_sides):
                when(entry[1], lambda: x_copy(n, side, y).wait_send())
            for side in range(2):
                pl.when(z_to[side])(lambda: z_copy(n, side, y).wait_send())
        for side in range(2):
            pl.when(y_to[side])(lambda: y_copy(n, side).wait_send())
    for m in range(4):
        pltpu.make_async_copy(ab.at[m, 0:ndev - 1], ab.at[m, 0:ndev - 1], a_send.at[m]).wait()
        pltpu.make_async_copy(ob.at[m], basis_hbm.at[m], out_sem.at[m]).wait()


def shards(mesh_sizes, rhs, blocks):
    nb, nr, lx, ly, lz = rhs.shape
    assert nb == 8 and nr == 8 and lx == 1 and lz == 128
    nx, ny, nz = mesh_sizes
    ndev = nx * ny * nz
    sides = max(1, min(2, nx - 1))
    rhs2 = rhs.reshape(nb * nr * ly, lz)
    blk2 = blocks.reshape(7, nb, nb * ly, lz)
    dma = pltpu.SemaphoreType.DMA
    vm = lambda *s: pltpu.VMEM(s, F32)
    basis, hess = pl.pallas_call(
        functools.partial(kernel, mesh_sizes, nb, nr, ly, lz),
        out_shape=(
            jax.ShapeDtypeStruct((ITERS + 1, nb * nr * ly, lz), F32),
            jax.ShapeDtypeStruct((32, 128), F32),
        ),
        in_specs=[pl.BlockSpec(memory_space=pl.ANY)] * 2,
        out_specs=(pl.BlockSpec(memory_space=pl.ANY), pl.BlockSpec(memory_space=pltpu.VMEM)),
        scratch_shapes=[
            vm(nb * nr * ly, lz),
            pltpu.VMEM((7, nb, nb * ly, lz), jnp.bfloat16),
            vm(ITERS, ly + 2, nb * 8, lz),
            vm(ly, nb * 8, lz),
            vm(ly, nb * 8, lz),
            vm(ITERS, sides, ly, nb * 8, lz),
            vm(ITERS, 2, ly, 8, lz),
            vm(ITERS, 2, ly, 8, lz),
            vm(5 + sides, ly, nb, nb * 8, lz),
            vm(2, nb * 8, lz),
            vm(ITERS + 1, ndev, 2, lz),
            vm(ITERS + 1, nb * nr * ly, lz),
            dma((ITERS, sides, ly)), dma((ITERS, sides, ly)),
            dma((ITERS, 2)), dma((ITERS, 2)),
            dma((ITERS, 2, ly)), dma((ITERS, 2, ly)),
            dma((ITERS + 1,)), dma((ITERS + 1,)),
            dma((2,)), dma((ITERS + 1,)),
            pltpu.SemaphoreType.REGULAR((2,)),
        ],
        compiler_params=pltpu.CompilerParams(collective_id=0, has_side_effects=True, vmem_limit_bytes=48 * 1024 * 1024),
    )(rhs2, blk2)
    basis = basis.reshape(ITERS + 1, nb, nr, lx, ly, lz)
    hess = hess[:24, :32].reshape(3, 8, 4, 8).transpose(2, 3, 0, 1)
    return basis, hess


def solution(mesh):
    sizes = tuple(mesh.shape[a] for a in AXES)
    return jax.shard_map(
        functools.partial(shards, sizes),
        mesh=mesh,
        in_specs=(P(None, None, "gx", "gy", "gz"), P(None, None, None, "gx", "gy", "gz")),
        out_specs=(P(None, None, None, "gx", "gy", "gz"), P()),
        check_vma=False,
    )
```

profile of v0, /device:TPU:0, one launch (start us, length us, event | category | flops | bytes accessed | tf_op | source)
XLA Modules:
  0.0 32.8 jit_solution(9028067164519100724)
XLA Ops:
  0.6 0.0 copy-start
  0.6 1.0 %copy-done = bf16[7,8,8,1,4,128]{5,4,3,2,1,0:T(4,128)(2,1)S(1)} copy-done((bf16[7,8,8,1,4,128]{5,4,3,2,1,0:T(4,128)(2,1)S(1)}, bf16[7,8,8,1,4,128]{5,4,3,2,1,0:T(4,128)(2,1)}, u32[]{:S(2)}) %copy-start) | copy-done | bytes 458776
  1.6 0.0 copy-start.1
  1.7 0.9 %copy-done.1 = f32[8,8,1,4,128]{4,3,2,1,0:T(4,128)S(1)} copy-done((f32[8,8,1,4,128]{4,3,2,1,0:T(4,128)S(1)}, f32[8,8,1,4,128]{4,3,2,1,0:T(4,128)}, u32[]{:S(2)}) %copy-start.1) | copy-done | bytes 131096
  2.6 28.7 %shard_map.41 = (f32[4,256,128]{2,1,0:T(8,128)S(1)}, f32[32,128]{1,0:T(8,128)S(1)}) custom-call(f32[256,128]{1,0:T(8,128)S(1)} %bitcast.8, bf16[7,8,32,128]{3,2,1,0:T(8,128)(2,1)S(1)} %bitcast.7), custom_call_target="tpu_custom_call" | custom-call | tf_op jit(solution)/shard_map/pallas_call | solution.py:381
  31.2 0.1 reshape.19
  31.3 0.7 %copy.4 = f32[3,8,4,8]{1,3,0,2:T(8,128)} copy(f32[3,8,4,8]{3,2,1,0:T(4,128)S(1)} %reshape.19) | data formatting | bytes 6144 | tf_op jit(solution)/shard_map/reshape | solution.py:412
  32.0 0.8 %copy.7 = f32[4,8,8,1,4,128]{5,4,3,2,1,0:T(4,128)} copy(f32[4,8,8,1,4,128]{5,4,3,2,1,0:T(4,128)S(1)} %bitcast.6) | data formatting | bytes 1048576
  (1 shorter events, 0.0 us)
Async XLA Ops:
  0.6 1.0 %copy-start = (bf16[7,8,8,1,4,128]{5,4,3,2,1,0:T(4,128)(2,1)S(1)}, bf16[7,8,8,1,4,128]{5,4,3,2,1,0:T(4,128)(2,1)}, u32[]{:S(2)}) copy-start(bf16[7,8,8,1,4,128]{5,4,3,2,1,0:T(4,128)(2,1)} %param.3) | copy-start | bytes 1376260
  1.6 0.9 %copy-start.1 = (f32[8,8,1,4,128]{4,3,2,1,0:T(4,128)S(1)}, f32[8,8,1,4,128]{4,3,2,1,0:T(4,128)}, u32[]{:S(2)}) copy-start(f32[8,8,1,4,128]{4,3,2,1,0:T(4,128)} %param.2) | copy-start | bytes 393220
where the time goes:
time: 33 us; the launch traced here: 32.8 us
  Pallas kernels  28.7 us (87%)
  local copies, waits for them, and re-layouts  3.5 us (11%)
  between operations  0.66 us (2%)
    pallas_call x1, Pallas kernels, shards(): pl.pallas_call(functools.partial(kernel, mesh_sizes, nb, nr, ly, lz), out...  28.7 us
    unnamed x5, local copies, waits for them, and re-layouts  2.71 us
    reshape x2, local copies, waits for them, and re-layouts, shards(): hess = hess[:24, :32].reshape(3, 8, 4, 8).transpose(2, 3, 0, 1)  0.79 us

commit v1 on v0

v1 whole, which is shorter than its diff:
```python
import functools

import jax
import jax.numpy as jnp
from jax import lax
from jax.experimental import pallas as pl
from jax.experimental.pallas import tpu as pltpu
from jax.sharding import PartitionSpec as P

ITERS = 3
F32 = jnp.float32
HIGH = lax.Precision.HIGHEST
AXES = ("gx", "gy", "gz")
MESH = pl.DeviceIdType.MESH


def dot_nt(a, b):
    return lax.dot_general(a, b, (((1,), (1,)), ((), ())), precision=HIGH, preferred_element_type=F32)


def dot_nn(a, b):
    return lax.dot_general(a, b, (((1,), (0,)), ((), ())), precision=HIGH, preferred_element_type=F32)


def tile_iota():
    row = lax.broadcasted_iota(jnp.int32, (8, 128), 0)
    lane = lax.broadcasted_iota(jnp.int32, (8, 128), 1)
    return row, lane


def empty():
    return jnp.zeros((8, 128), F32)


def pad_rows(pieces):
    return jnp.concatenate(pieces + [empty()] * (16 - len(pieces)), axis=0)


def spread(ref, index, r):
    return jnp.broadcast_to(ref[index + (pl.ds(r, 1), slice(None))], (8, 128))


def column(m, c):
    return jnp.broadcast_to(m[:, c:c + 1], (8, 128))


def cholesky(s, aug, base, row, lane):
    cols = [column(s, c) for c in range(8)]
    low = empty()
    for k in range(8):
        piv = jnp.broadcast_to(cols[k][k:k + 1], (8, 128))
        rs = lax.rsqrt(piv)
        rs = rs * (1.5 - 0.5 * piv * rs * rs)
        lk = jnp.where(row >= k, cols[k] * rs, 0.0)
        low = low + jnp.where(lane == base + k, lk, 0.0)
        arow = jnp.broadcast_to(aug[k:k + 1], (8, 128)) * rs
        aug = jnp.where(row == k, arow, aug - jnp.where(row > k, lk, 0.0) * arow)
        for c in range(k + 1, 8):
            cols[c] = cols[c] - lk * jnp.broadcast_to(lk[c:c + 1], (8, 128))
    return low, aug


def krylov(
    mesh_sizes, nb, nr, ly, lz,
    rhs_hbm, blk_hbm, q_ref, p3, small,
    rv, bv, cf, vp, p1, p2, xb, xg, zs, zr, zp, loc, aa, ab, ac,
    x_send, x_recv, y_send, y_recv, z_send, z_recv, a_send, a_recv, in_sem, known,
):
    nx, ny, nz = mesh_sizes
    ndev = nx * ny * nz
    gx, gy, gz = (lax.axis_index(a) for a in AXES)
    me = (gx * ny + gy) * nz + gz
    cells = ndev * ly * lz
    row, lane = tile_iota()
    barrier = pltpu.get_barrier_semaphore()

    in_rhs = pltpu.make_async_copy(rhs_hbm, rv, in_sem.at[7])
    in_rhs.start()
    terms = [0, 3, 4, 5, 6, 1, 2]
    in_blk = [pltpu.make_async_copy(blk_hbm.at[k], bv.at[k], in_sem.at[k]) for k in range(7)]
    for k in terms:
        in_blk[k].start()

    def wrapped(at, d, size):
        t = at + d
        return jnp.where(t >= size, t - size, t)

    def greet(sem, axis):
        size, at = {"gx": (nx, gx), "gy": (ny, gy), "gz": (nz, gz)}[axis]
        if size <= 8:
            for d in range(1, size):
                pl.semaphore_signal(sem, inc=1, device_id={axis: wrapped(at, d, size)}, device_id_type=MESH)
        else:
            def body(d, c):
                pl.semaphore_signal(sem, inc=1, device_id={axis: lax.rem(at + d, size)}, device_id_type=MESH)
                return c
            lax.fori_loop(1, size, body, 0)

    for axis in AXES[::-1]:
        greet(barrier, axis)

    if nx == 1:
        x_sides = []
    elif nx == 2:
        x_sides = [(1 + gx, None, 1 - gx)]
    else:
        x_sides = [(1, gx < nx - 1, gx + 1), (2, gx > 0, gx - 1)]

    def when(cond, fn):
        if cond is None:
            fn()
        else:
            pl.when(cond)(fn)

    def remote(src, dst, ssem, rsem, dev):
        return pltpu.make_async_remote_copy(
            src_ref=src, dst_ref=dst, send_sem=ssem, recv_sem=rsem, device_id=dev, device_id_type=MESH)

    def x_copy(n, side, y):
        opposite = side if nx == 2 else 1 - side
        return remote(vp.at[n, 1 + y], xb.at[n, opposite, y], x_send.at[n, side, y],
                      x_recv.at[n, opposite, y], {"gx": x_sides[side][2]})

    def x_arrived(n, side, y):
        remote(vp.at[n, 1 + y], xb.at[n, side, y], x_send.at[n, side, y],
               x_recv.at[n, side, y], {"gx": x_sides[side][2]}).wait_recv()

    def y_copy(n, side):
        if side == 0:
            return remote(vp.at[n, ly], vp.at[n, 0], y_send.at[n, 0], y_recv.at[n, 0], {"gy": gy + 1})
        return remote(vp.at[n, 1], vp.at[n, ly + 1], y_send.at[n, 1], y_recv.at[n, 1], {"gy": gy - 1})

    def z_copy(n, side, y):
        target = gz - 1 if side == 0 else gz + 1
        return remote(zs.at[n, y], zr.at[n, side, y], z_send.at[n, side, y], z_recv.at[n, side, y], {"gz": target})

    y_to = (gy < ny - 1, gy > 0)
    y_from = (gy > 0, gy < ny - 1)
    z_to = (gz > 0, gz < nz - 1)
    z_from = (gz < nz - 1, gz > 0)

    for side in range(2):
        @pl.when(jnp.logical_not(y_from[side]))
        def _():
            for n in range(ITERS):
                vp[n, 0 if side == 0 else ly + 1] = jnp.zeros((nb * 8, 128), F32)

        @pl.when(jnp.logical_not(z_from[side]))
        def _():
            for n in range(ITERS):
                zr[n, side] = jnp.zeros((ly, 8, 128), F32)

    if nx > 2:
        for side in range(2):
            @pl.when(jnp.logical_not(x_sides[side][1]))
            def _():
                for n in range(ITERS):
                    xb[n, side] = jnp.zeros((ly, nb * 8, 128), F32)

    def send_x(n, y):
        for side, entry in enumerate(x_sides):
            when(entry[1], lambda: x_copy(n, side, y).start())

    def send_yz(n, y):
        if y == ly - 1:
            pl.when(y_to[0])(lambda: y_copy(n, 0).start())
        if y == 0:
            pl.when(y_to[1])(lambda: y_copy(n, 1).start())
        edge = empty()
        for a in range(nb):
            v = vp[n, 1 + y, a * 8:(a + 1) * 8]
            edge = jnp.where(lane // 2 == a, pltpu.roll(v, 2 * a + 1, 1), edge)
        zs[n, y] = edge
        for side in range(2):
            pl.when(z_to[side])(lambda: z_copy(n, side, y).start())

    order = [0] + ([ly - 1] if ly > 1 else []) + list(range(1, ly - 1))

    in_rhs.wait()
    for y in order:
        for a in range(nb):
            vp[0, 1 + y, a * 8:(a + 1) * 8] = rv[pl.ds(a * nr * ly + y, 8, stride=ly), :]
    pl.semaphore_wait(barrier, nx + ny + nz - 3)
    for y in order:
        send_x(0, y)
    greet(known.at[0], "gy")
    for y in order:
        send_yz(0, y)

    def convert(k, total):
        def body(i, total):
            rows = bv[k, i].astype(F32)
            cf[k, i] = rows
            for r in range(0, nb * ly, 8):
                total = total + jnp.abs(rows[r:r + 8])
            return total
        return lax.fori_loop(0, nb, body, total)

    total_abs = empty()
    for k in terms:
        in_blk[k].wait()
        total_abs = convert(k, total_abs)
    trace = jnp.zeros((ly, 128), F32)
    for i in range(nb):
        trace = trace + cf[0, i, i * ly:(i + 1) * ly]

    views = [(vp, (0,), 1), (p1, (), 0), (p2, (), 1), (p3, (), 0)]

    def tile(i, y, a):
        ref, index, off = views[i]
        return ref[index + (off + y, pl.ds(pl.multiple_of(a * 8, 8), 8), slice(None))]

    def tile_row(i, y, r):
        ref, index, off = views[i]
        return spread(ref, index + (off + y,), r)

    def gram_row(n, y, acc):
        def body(a, acc):
            p = tile(n, y, a)
            return tuple(acc[i * 8 + s] + p * tile_row(i, y, a * 8 + s)
                         for i in range(n + 1) for s in range(8))
        return lax.fori_loop(0, nb, body, acc)

    def gram_zero(n):
        return tuple(empty() for _ in range(8 * (n + 1)))

    def gram_end(acc, width):
        d = empty()
        for k, part in enumerate(acc):
            d = jnp.where(lane % width == k, jnp.sum(part, axis=1, keepdims=True), d)
        return d

    def gram(n):
        acc = gram_zero(n)
        for y in range(ly):
            acc = gram_row(n, y, acc)
        return acc

    def pack32(d):
        d = jnp.where(lane // 32 == row % 4, d, 0.0)
        return [jnp.sum(d[0:4], axis=0, keepdims=True), jnp.sum(d[4:8], axis=0, keepdims=True)]

    def pack16(d):
        d = jnp.where(lane // 16 == row, d, 0.0)
        return [jnp.sum(d, axis=0, keepdims=True)]

    def unpack32(t0, t1):
        z = jnp.where(row < 4, t0, t1)
        out = z
        for g in range(1, 4):
            out = jnp.where(row % 4 == g, pltpu.roll(z, 128 - 32 * g, 1), out)
        return out

    def unpack16(t):
        z = jnp.broadcast_to(t, (8, 128))
        out = z
        for g in range(1, 8):
            out = jnp.where(row == g, pltpu.roll(z, 128 - 16 * g, 1), out)
        return out

    def far(i, n):
        return min(i, n - i)

    offsets = [(dx, dy, dz) for dx in range(nx) for dy in range(ny) for dz in range(nz) if dx or dy or dz]
    offsets.sort(key=lambda o: -(far(o[0], nx) + far(o[1], ny) + far(o[2], nz)))

    def ar_start(buf, m, rows):
        for r, v in enumerate(rows):
            buf[me, r:r + 1] = v
        if ndev <= 64:
            xs = [wrapped(gx, d, nx) for d in range(nx)]
            ys = [wrapped(gy, d, ny) for d in range(ny)]
            zs_ = [wrapped(gz, d, nz) for d in range(nz)]
            for dx, dy, dz in offsets:
                remote(buf.at[me], buf.at[me], a_send.at[m], a_recv.at[m], (xs[dx], ys[dy], zs_[dz])).start()
        else:
            def body(d, c):
                t = lax.rem(me + d, ndev)
                remote(buf.at[me], buf.at[me], a_send.at[m], a_recv.at[m],
                       (t // (ny * nz), (t // nz) % ny, t % nz)).start()
                return c
            lax.fori_loop(1, ndev, body, 0)

    def ar_wait(buf, sem):
        pltpu.make_async_copy(buf.at[0:ndev - 1], buf.at[0:ndev - 1], sem).wait()

    def ar_done(buf, m):
        ar_wait(buf, a_recv.at[m])
        return jnp.sum(buf[...], axis=0)

    lane_sum = lambda x: jnp.sum(x, axis=1, keepdims=True)
    pl.semaphore_wait(known.at[0], ny - 1)
    greet(known.at[1], "gx")
    d0 = gram_end(gram(0), 32)
    d0 = d0 + jnp.where(lane % 32 == 8, jnp.where(row < ly, lane_sum(jnp.concatenate(
        [trace, jnp.zeros((8 - ly, 128), F32)], axis=0)), 0.0), 0.0)
    d0 = d0 + jnp.where(lane % 32 == 9, lane_sum(total_abs), 0.0)
    pl.semaphore_wait(known.at[1], nx - 1)
    ar_start(aa, 0, pack32(d0))

    def halos(n):
        for side in range(2):
            @pl.when(z_from[side])
            def _():
                for y in range(ly):
                    z_copy(n, side, y).wait_recv()
            pl.when(y_from[side])(lambda: y_copy(n, side).wait_recv())

    def local_rows(n, field, off, edges):
        for y in order:
            plus, minus = edges(y)
            for j in range(nb):
                v = field(off + y, j)
                zp[y, 0, j * 8:(j + 1) * 8] = jnp.where(
                    lane == lz - 1, pltpu.roll(plus, lz - 2 - 2 * j, 1), pltpu.roll(v, lz - 1, 1))
                zp[y, 1, j * 8:(j + 1) * 8] = jnp.where(
                    lane == 0, pltpu.roll(minus, lz - 2 * j, 1) if j else minus, pltpu.roll(v, 1, 1))
        for y in order:
            def body(j, acc):
                at = pl.ds(pl.multiple_of(j * 8, 8), 8)
                values = [field(off + y, j), field(off + y + 1, j), field(off + y - 1, j), zp[y, 0, at, :], zp[y, 1, at, :]]
                acc = list(acc)
                for k, v in zip(terms, values):
                    for i in range(nb):
                        acc[i] = acc[i] + spread(cf, (k, i), j * ly + y) * v
                return tuple(acc)
            acc = lax.fori_loop(0, nb, body, tuple(empty() for _ in range(nb)))
            for i in range(nb):
                loc[y, i * 8:(i + 1) * 8] = acc[i]

    def x_terms(n, y, value):
        acc = tuple(loc[y, i * 8:(i + 1) * 8] for i in range(nb))
        for side, entry in enumerate(x_sides):
            when(entry[1], lambda: x_arrived(n, side, y))
            k = entry[0]

            def body(j, acc):
                v = value(side, y, pl.ds(pl.multiple_of(j * 8, 8), 8))
                return tuple(acc[i] + spread(cf, (k, i), j * ly + y) * v for i in range(nb))
            acc = lax.fori_loop(0, nb, body, acc)
        return acc

    for n in range(ITERS - 1):
        halos(n)
        local_rows(n, lambda y, j: vp[n, y, pl.ds(pl.multiple_of(j * 8, 8), 8), :], 1,
                   lambda y: (zr[n, 0, y], zr[n, 1, y]))
        for y in order:
            acc = x_terms(n, y, lambda side, y, at: xb[n, side, y, at, :])
            for i in range(nb):
                vp[n + 1, 1 + y, i * 8:(i + 1) * 8] = acc[i]
            send_x(n + 1, y)
            send_yz(n + 1, y)

    sums = ar_done(aa, 0)
    red0 = unpack32(sums[0:1], sums[1:2])
    sigma = jnp.broadcast_to(lane_sum(jnp.where((row < ly) & (lane == 8), red0, 0.0)), (8, 128))
    sigma = jnp.broadcast_to(jnp.sum(sigma, axis=0, keepdims=True), (8, 128)) / (8.0 * cells)
    nu = jnp.broadcast_to(lane_sum(jnp.where(lane == 9, red0, 0.0)), (8, 128))
    nu = jnp.broadcast_to(jnp.sum(nu, axis=0, keepdims=True), (8, 128)) / (8.0 * cells)
    inv = 1.0 / nu
    sig1, inv1 = sigma[0:1], inv[0:1]

    def shift1(v0, v1):
        return (v1 - sig1 * v0) * inv1

    def shift2(v0, v1, v2):
        return ((v2 - sig1 * v1) * inv1 - sig1 * shift1(v0, v1)) * inv1

    for y in range(ly):
        p1[y] = shift1(vp[0, 1 + y], vp[1, 1 + y])
        p2[1 + y] = shift2(vp[0, 1 + y], vp[1, 1 + y], vp[2, 1 + y])
    g1 = gram_end(gram(1), 16)
    g2 = gram_end(gram(2), 32)
    ar_start(ab, 1, pack32(g2) + pack16(g1) + [jnp.zeros((1, 128), F32)])

    for side in range(len(x_sides)):
        for y in range(ly):
            xg[side, y] = sig1 * xb[1, side, y] * inv1 + sig1 * shift1(xb[0, side, y], xb[1, side, y])
    halos(2)
    for h in (0, ly + 1):
        p2[h] = shift2(vp[0, h], vp[1, h], vp[2, h])
    local_rows(2, lambda y, j: p2[y, pl.ds(pl.multiple_of(j * 8, 8), 8), :], 1,
               lambda y: tuple(shift2(zr[0, s, y], zr[1, s, y], zr[2, s, y]) for s in range(2)))
    acc3 = gram_zero(3)
    for y in order:
        acc = x_terms(2, y, lambda side, y, at: (xb[2, side, y, at, :] * inv1 - xg[side, y, at, :]) * inv1)
        for i in range(nb):
            p3[y, i * 8:(i + 1) * 8] = (acc[i] - sig1 * p2[1 + y, i * 8:(i + 1) * 8]) * inv1
        acc3 = gram_row(3, y, acc3)
    ar_start(ac, 2, pack32(gram_end(acc3, 32)))

    weights, factors = [], []

    def factor(n, red):
        base = 8 * n
        unit = jnp.where(lane == base + row, 1.0, 0.0).astype(F32)
        d = jnp.where(lane < base + 8, red, 0.0)
        if n:
            rt = dot_nt(d, pad_rows(weights))
            s = pltpu.roll(d, 128 - base, 1) - dot_nt(rt, pad_rows([rt]))
            low, aug = cholesky(s, unit - rt, base, row, lane)
            weights.append(dot_nn(aug, pad_rows(weights + [unit])))
            factors.append(rt + low)
        else:
            low, aug = cholesky(d, unit, base, row, lane)
            weights.append(aug)
            factors.append(low)

    def emit(n):
        cols = [column(weights[n], c) for c in range(8 * (n + 1))]

        def body(a, c):
            for y in range(ly):
                parts = []
                for i in range(n + 1):
                    part = None
                    for s in range(8):
                        t = cols[i * 8 + s] * tile_row(i, y, a * 8 + s)
                        part = t if part is None else part + t
                    parts.append(part)
                q_ref[n, pl.ds(a * nr * ly + y, 8, stride=ly), :] = sum(parts[1:], parts[0])
            return c
        lax.fori_loop(0, nb, body, 0)

    factor(0, red0)
    emit(0)
    sums = ar_done(ab, 1)
    factor(1, unpack16(sums[2:3]))
    emit(1)
    factor(2, unpack32(sums[0:1], sums[1:2]))
    emit(2)

    small[8:32] = jnp.concatenate(weights, axis=0)
    small[32:40] = factors[1]
    small[40:48] = factors[2]
    small[48:56] = sigma
    small[56:64] = nu
    for n in range(ITERS):
        for side, entry in enumerate(x_sides):
            def sent():
                for y in range(ly):
                    x_copy(n, side, y).wait_send()
            when(entry[1], sent)
        for side in range(2):
            @pl.when(z_to[side])
            def _():
                for y in range(ly):
                    z_copy(n, side, y).wait_send()
            pl.when(y_to[side])(lambda: y_copy(n, side).wait_send())
    for m, buf in enumerate((aa, ab, ac)):
        ar_wait(buf, a_send.at[m])
    sums = ar_done(ac, 2)
    small[0:8] = unpack32(sums[0:1], sums[1:2])


def finish(nb, nr, ly, q_ref, p3, small, basis_hbm, hess_hbm, rest, ob, hs, sem, hsem):
    row, lane = tile_iota()
    early = [pltpu.make_async_copy(q_ref.at[n], basis_hbm.at[n], sem.at[n]) for n in range(ITERS)]
    for copy in early:
        copy.start()
    base = 8 * ITERS
    d = jnp.where(lane < base + 8, small[0:8], 0.0)
    weights = [small[8 * (n + 1):8 * (n + 2)] for n in range(ITERS)]
    rt = dot_nt(d, pad_rows(weights))
    s = pltpu.roll(d, 128 - base, 1) - dot_nt(rt, pad_rows([rt]))
    cols = [column(rt, c) for c in range(base)]
    for a in range(nb):
        for y in range(ly):
            parts = [p3[y, a * 8:(a + 1) * 8]]
            for i in range(ITERS):
                part = None
                for t in range(8):
                    u = cols[i * 8 + t] * spread(q_ref, (i,), a * nr * ly + t * ly + y)
                    part = u if part is None else part + u
                parts.append(part)
            rest[y, a * 8:(a + 1) * 8] = parts[0] - ((parts[1] + parts[2]) + parts[3])
    unit = jnp.where(lane == row, 1.0, 0.0).astype(F32)
    low, inverse = cholesky(s, unit, base, row, lane)
    cols = [column(inverse, c) for c in range(8)]
    late = []
    half = nb // 2
    for h in range(2):
        for a in range(h * half, (h + 1) * half):
            for y in range(ly):
                part = [cols[t] * spread(rest, (y,), a * 8 + t) for t in range(8)]
                total = ((part[0] + part[1]) + (part[2] + part[3])) + ((part[4] + part[5]) + (part[6] + part[7]))
                ob[pl.ds(a * nr * ly + y, 8, stride=ly), :] = total
        at = pl.ds(h * half * nr * ly, half * nr * ly)
        copy = pltpu.make_async_copy(ob.at[at], basis_hbm.at[ITERS, at], sem.at[ITERS + h])
        copy.start()
        late.append(copy)
    factors = [small[32:40], small[40:48], rt + low]
    h = dot_nn(jnp.concatenate(weights + [empty()], axis=0), pad_rows(factors))
    hr = lax.broadcasted_iota(jnp.int32, (32, 128), 0)
    hl = lax.broadcasted_iota(jnp.int32, (32, 128), 1)
    h = h * small[56:57] + jnp.where(hr == hl, small[48:49], 0.0)
    t = jnp.concatenate([h, jnp.zeros((96, 128), F32)], axis=0).T
    for i in range(ITERS + 1):
        for j in range(ITERS):
            hs[i, j] = t[8 * i:8 * i + 8, 8 * j:8 * j + 8]
    copy = pltpu.make_async_copy(hs, hess_hbm, hsem)
    copy.start()
    for c in early + late + [copy]:
        c.wait()


def shards(mesh_sizes, rhs, blocks):
    nb, nr, lx, ly, lz = rhs.shape
    assert nb == 8 and nr == 8 and lx == 1 and lz == 128 and ly <= 8
    nx, ny, nz = mesh_sizes
    ndev = nx * ny * nz
    sides = max(1, min(2, nx - 1))
    rhs2 = pltpu.with_memory_space_constraint(rhs.reshape(nb * nr * ly, lz), pltpu.HBM)
    blk2 = pltpu.with_memory_space_constraint(blocks.reshape(7, nb, nb * ly, lz), pltpu.HBM)
    dma = pltpu.SemaphoreType.DMA
    vm = lambda *s: pltpu.VMEM(s, F32)
    hbm = pl.BlockSpec(memory_space=pltpu.HBM)
    vmem = pl.BlockSpec(memory_space=pltpu.VMEM)
    q, p3, small = pl.pallas_call(
        functools.partial(krylov, mesh_sizes, nb, nr, ly, lz),
        out_shape=(
            jax.ShapeDtypeStruct((ITERS, nb * nr * ly, lz), F32),
            jax.ShapeDtypeStruct((ly, nb * 8, lz), F32),
            jax.ShapeDtypeStruct((64, lz), F32),
        ),
        in_specs=[hbm] * 2,
        out_specs=(vmem,) * 3,
        scratch_shapes=[
            vm(nb * nr * ly, lz),
            pltpu.VMEM((7, nb, nb * ly, lz), jnp.bfloat16),
            vm(7, nb, nb * ly, lz),
            vm(ITERS, ly + 2, nb * 8, lz),
            vm(ly, nb * 8, lz),
            vm(ly + 2, nb * 8, lz),
            vm(ITERS, sides, ly, nb * 8, lz),
            vm(sides, ly, nb * 8, lz),
            vm(ITERS, ly, 8, lz),
            vm(ITERS, 2, ly, 8, lz),
            vm(ly, 2, nb * 8, lz),
            vm(ly, nb * 8, lz),
            vm(ndev, 2, lz), vm(ndev, 4, lz), vm(ndev, 2, lz),
            dma((ITERS, sides, ly)), dma((ITERS, sides, ly)),
            dma((ITERS, 2)), dma((ITERS, 2)),
            dma((ITERS, 2, ly)), dma((ITERS, 2, ly)),
            dma((3,)), dma((3,)),
            dma((8,)),
            pltpu.SemaphoreType.REGULAR((2,)),
        ],
        compiler_params=pltpu.CompilerParams(collective_id=0, has_side_effects=True, vmem_limit_bytes=48 * 1024 * 1024),
    )(rhs2, blk2)
    basis, hess = pl.pallas_call(
        functools.partial(finish, nb, nr, ly),
        out_shape=(
            jax.ShapeDtypeStruct((ITERS + 1, nb * nr * ly, lz), F32),
            jax.ShapeDtypeStruct((ITERS + 1, ITERS, 8, 8), F32),
        ),
        in_specs=[vmem] * 3,
        out_specs=(hbm,) * 2,
        scratch_shapes=[
            vm(ly, nb * 8, lz),
            vm(nb * nr * ly, lz),
            vm(ITERS + 1, ITERS, 8, 8),
            dma((ITERS + 2,)),
            dma,
        ],
        compiler_params=pltpu.CompilerParams(vmem_limit_bytes=8 * 1024 * 1024),
    )(q, p3, small)
    return basis.reshape(ITERS + 1, nb, nr, lx, ly, lz), hess.transpose(0, 2, 1, 3)


def solution(mesh):
    sizes = tuple(mesh.shape[a] for a in AXES)
    return jax.shard_map(
        functools.partial(shards, sizes),
        mesh=mesh,
        in_specs=(P(None, None, "gx", "gy", "gz"), P(None, None, None, "gx", "gy", "gz")),
        out_specs=(P(None, None, None, "gx", "gy", "gz"), P()),
        check_vma=False,
    )
```

time: 33 us -> 27.6 us (0.84)
  local copies, waits for them, and re-layouts: 3.5 us -> 0 us
  Pallas kernels: 28.7 us -> 26.8 us
    unnamed x5 -> x0, local copies, waits for them, and re-layouts: 2.71 us -> none
    pallas_call x1 -> x2, Pallas kernels: 28.7 us -> 26.8 us  [the longest x1 25.4 us: shards(): pl.pallas_call(functools.partial(krylov, mesh_sizes, nb, nr, ly, lz), out...]
    reshape x2 -> x0, local copies, waits for them, and re-layouts: 0.79 us -> none  [shards(): hess = hess[:24, :32].reshape(3, 8, 4, 8).transpose(2, 3, 0, 1)]
where the time goes in v1:
time: 27.6 us; the launch traced here: 27.5 us
  Pallas kernels  26.8 us (97%)
  between operations  0.64 us (2%)
    pallas_call x1, Pallas kernels, shards(): pl.pallas_call(functools.partial(krylov, mesh_sizes, nb, nr, ly, lz), out...  25.4 us
    pallas_call x1, Pallas kernels, shards(): pl.pallas_call(functools.partial(finish, nb, nr, ly), out_shape=(jax.Shap...  1.46 us

profile of v1, /device:TPU:0, one launch (start us, length us, event | category | flops | bytes accessed | tf_op | source)
XLA Modules:
  0.0 27.5 jit_solution(5837425910947603065)
XLA Ops:
  0.6 25.4 %shard_map.41 = (f32[3,256,128]{2,1,0:T(8,128)S(1)}, f32[4,64,128]{2,1,0:T(8,128)S(1)}, f32[64,128]{1,0:T(8,128)S(1)}) custom-call(f32[256,128]{1,0:T(8,128)} %bitcast.7, bf16[7,8,32,128]{3,2,1,0:T(8,128)(2,1)} %bitcast.6), custom_call_target="tpu_custom_call" | custom-call | tf_op jit(solution)/shard_map/pallas_call | solution.py:519
  26.0 1.5 %shard_map.42 = (f32[4,256,128]{2,1,0:T(8,128)}, f32[4,3,8,8]{3,2,1,0:T(8,128)}) custom-call(f32[3,256,128]{2,1,0:T(8,128)S(1)} %get-tuple-element.7.q_ref, f32[4,64,128]{2,1,0:T(8,128)S(1)} %get-tuple-element.8.p3, f32[64,128]{1,0:T(8,128)S(1)} %get-tuple-element.9.small), custom_call_target="tpu_custom_call" | custom-call | tf_op jit(solution)/shard_map/pallas_call | solution.py:551

commit v2 on v1

--- a/solution.py
+++ b/solution.py
@@ -44,26 +44,26 @@
     return jnp.broadcast_to(m[:, c:c + 1], (8, 128))
 
 
-def cholesky(s, aug, base, row, lane):
+def cholesky(s, aug, row, lane):
     cols = [column(s, c) for c in range(8)]
-    low = empty()
+    lower = []
     for k in range(8):
         piv = jnp.broadcast_to(cols[k][k:k + 1], (8, 128))
         rs = lax.rsqrt(piv)
         rs = rs * (1.5 - 0.5 * piv * rs * rs)
         lk = jnp.where(row >= k, cols[k] * rs, 0.0)
-        low = low + jnp.where(lane == base + k, lk, 0.0)
+        lower.append(lk)
         arow = jnp.broadcast_to(aug[k:k + 1], (8, 128)) * rs
         aug = jnp.where(row == k, arow, aug - jnp.where(row > k, lk, 0.0) * arow)
         for c in range(k + 1, 8):
             cols[c] = cols[c] - lk * jnp.broadcast_to(lk[c:c + 1], (8, 128))
-    return low, aug
+    return lower, aug
 
 
 def krylov(
     mesh_sizes, nb, nr, ly, lz,
     rhs_hbm, blk_hbm, q_ref, p3, small,
-    rv, bv, cf, vp, p1, p2, xb, xg, zs, zr, zp, loc, aa, ab, ac,
+    rv, bv, cf, cz, vp, p1, p2, xb, xg, zs, zr, zp, hz, loc, aa, ab, ac,
     x_send, x_recv, y_send, y_recv, z_send, z_recv, a_send, a_recv, in_sem, known,
 ):
     nx, ny, nz = mesh_sizes
@@ -74,12 +74,10 @@
     row, lane = tile_iota()
     barrier = pltpu.get_barrier_semaphore()
 
-    in_rhs = pltpu.make_async_copy(rhs_hbm, rv, in_sem.at[7])
+    in_rhs = pltpu.make_async_copy(rhs_hbm, rv, in_sem.at[0])
+    in_blk = pltpu.make_async_copy(blk_hbm, bv, in_sem.at[1])
     in_rhs.start()
-    terms = [0, 3, 4, 5, 6, 1, 2]
-    in_blk = [pltpu.make_async_copy(blk_hbm.at[k], bv.at[k], in_sem.at[k]) for k in range(7)]
-    for k in terms:
-        in_blk[k].start()
+    in_blk.start()
 
     def wrapped(at, d, size):
         t = at + d
@@ -118,21 +116,28 @@
 
     def x_copy(n, side, y):
         opposite = side if nx == 2 else 1 - side
-        return remote(vp.at[n, 1 + y], xb.at[n, opposite, y], x_send.at[n, side, y],
-                      x_recv.at[n, opposite, y], {"gx": x_sides[side][2]})
+        return remote(vp.at[n, 1 + y], xb.at[n, opposite, y], x_send.at[side],
+                      x_recv.at[n % 2, opposite, y], {"gx": x_sides[side][2]})
 
     def x_arrived(n, side, y):
-        remote(vp.at[n, 1 + y], xb.at[n, side, y], x_send.at[n, side, y],
-               x_recv.at[n, side, y], {"gx": x_sides[side][2]}).wait_recv()
+        remote(vp.at[n, 1 + y], xb.at[n, side, y], x_send.at[side],
+               x_recv.at[n % 2, side, y], {"gx": x_sides[side][2]}).wait_recv()
 
     def y_copy(n, side):
         if side == 0:
-            return remote(vp.at[n, ly], vp.at[n, 0], y_send.at[n, 0], y_recv.at[n, 0], {"gy": gy + 1})
-        return remote(vp.at[n, 1], vp.at[n, ly + 1], y_send.at[n, 1], y_recv.at[n, 1], {"gy": gy - 1})
+            return remote(vp.at[n, ly], vp.at[n, 0], y_send.at[0], y_recv.at[n % 2, 0], {"gy": gy + 1})
+        return remote(vp.at[n, 1], vp.at[n, ly + 1], y_send.at[1], y_recv.at[n % 2, 1], {"gy": gy - 1})
 
     def z_copy(n, side, y):
         target = gz - 1 if side == 0 else gz + 1
-        return remote(zs.at[n, y], zr.at[n, side, y], z_send.at[n, side, y], z_recv.at[n, side, y], {"gz": target})
+        return remote(zs.at[n, y], zr.at[n, y, side], z_send.at[side], z_recv.at[n % 2, y], {"gz": target})
+
+    def take(ref, sem):
+        pltpu.make_async_copy(ref, ref, sem).wait()
+
+    def z_arrived(n, y):
+        pl.when(jnp.logical_and(z_from[0], z_from[1]))(lambda: take(zr.at[n, y], z_recv.at[n % 2, y]))
+        pl.when(z_from[0] != z_from[1])(lambda: take(zr.at[n, y, 0], z_recv.at[n % 2, y]))
 
     y_to = (gy < ny - 1, gy > 0)
     y_from = (gy > 0, gy < ny - 1)
@@ -148,7 +153,8 @@
         @pl.when(jnp.logical_not(z_from[side]))
         def _():
             for n in range(ITERS):
-                zr[n, side] = jnp.zeros((ly, 8, 128), F32)
+                for y in range(ly):
+                    zr[n, y, side] = empty()
 
     if nx > 2:
         for side in range(2):
@@ -187,22 +193,41 @@
     for y in order:
         send_yz(0, y)
 
-    def convert(k, total):
-        def body(i, total):
+    def shifted(i, y, v):
+        zp[y, 0, i * 8:(i + 1) * 8] = pltpu.roll(v, lz - 1, 1)
+        zp[y, 1, i * 8:(i + 1) * 8] = pltpu.roll(v, 1, 1)
+
+    for y in order:
+        for j in range(nb):
+            shifted(j, y, vp[0, 1 + y, j * 8:(j + 1) * 8])
+
+    in_blk.wait()
+
+    def absolute(rows, total):
+        for r in range(0, nb * ly, 8):
+            total = total + jnp.abs(rows[r:r + 8])
+        return total
+
+    def convert(i, total):
+        for k in (0, 1, 2, 3, 4):
             rows = bv[k, i].astype(F32)
             cf[k, i] = rows
-            for r in range(0, nb * ly, 8):
-                total = total + jnp.abs(rows[r:r + 8])
-            return total
-        return lax.fori_loop(0, nb, body, total)
-
-    total_abs = empty()
-    for k in terms:
-        in_blk[k].wait()
-        total_abs = convert(k, total_abs)
+            total = absolute(rows, total)
+        plus, minus = bv[5, i].astype(F32), bv[6, i].astype(F32)
+        total = absolute(minus, absolute(plus, total))
+        at = lax.broadcasted_iota(jnp.int32, (nb * ly, 128), 1)
+        cf[5, i] = jnp.where(at == lz - 1, 0.0, plus)
+        cf[6, i] = jnp.where(at == 0, 0.0, minus)
+        cz[i] = jnp.where(at == lz - 1, plus, jnp.where(at == 0, minus, 0.0))
+        return total
+
+    total_abs = lax.fori_loop(0, nb, convert, empty())
     trace = jnp.zeros((ly, 128), F32)
     for i in range(nb):
         trace = trace + cf[0, i, i * ly:(i + 1) * ly]
+
+    def pairs(body, acc):
+        return lax.fori_loop(0, nb // 2, lambda t, acc: body(2 * t + 1, body(2 * t, acc)), acc)
 
     views = [(vp, (0,), 1), (p1, (), 0), (p2, (), 1), (p3, (), 0)]
 
@@ -219,7 +244,7 @@
             p = tile(n, y, a)
             return tuple(acc[i * 8 + s] + p * tile_row(i, y, a * 8 + s)
                          for i in range(n + 1) for s in range(8))
-        return lax.fori_loop(0, nb, body, acc)
+        return pairs(body, acc)
 
     def gram_zero(n):
         return tuple(empty() for _ in range(8 * (n + 1)))
@@ -258,21 +283,21 @@
             out = jnp.where(row == g, pltpu.roll(z, 128 - 16 * g, 1), out)
         return out
 
-    def far(i, n):
-        return min(i, n - i)
-
-    offsets = [(dx, dy, dz) for dx in range(nx) for dy in range(ny) for dz in range(nz) if dx or dy or dz]
-    offsets.sort(key=lambda o: -(far(o[0], nx) + far(o[1], ny) + far(o[2], nz)))
+    def ends(at, size):
+        return [jnp.where(2 * at < size, size - 1 - k, k) for k in range(size)]
 
     def ar_start(buf, m, rows):
         for r, v in enumerate(rows):
             buf[me, r:r + 1] = v
         if ndev <= 64:
-            xs = [wrapped(gx, d, nx) for d in range(nx)]
-            ys = [wrapped(gy, d, ny) for d in range(ny)]
-            zs_ = [wrapped(gz, d, nz) for d in range(nz)]
-            for dx, dy, dz in offsets:
-                remote(buf.at[me], buf.at[me], a_send.at[m], a_recv.at[m], (xs[dx], ys[dy], zs_[dz])).start()
+            xs = [wrapped(gx, nx - 1 - d, nx) for d in range(nx)]
+            ys = [wrapped(gy, (d + ny // 2) % ny, ny) for d in range(ny)]
+            for z in ends(gz, nz):
+                for dx in range(nx):
+                    for dy in range(ny):
+                        copy = remote(buf.at[me], buf.at[me], a_send.at[m], a_recv.at[m], (xs[dx], ys[dy], z))
+                        own = dx == nx - 1 and (dy + ny // 2) % ny == 0
+                        when(z != gz if own else None, copy.start)
         else:
             def body(d, c):
                 t = lax.rem(me + d, ndev)
@@ -281,11 +306,8 @@
                 return c
             lax.fori_loop(1, ndev, body, 0)
 
-    def ar_wait(buf, sem):
-        pltpu.make_async_copy(buf.at[0:ndev - 1], buf.at[0:ndev - 1], sem).wait()
-
     def ar_done(buf, m):
-        ar_wait(buf, a_recv.at[m])
+        take(buf.at[0:ndev - 1], a_recv.at[m])
         return jnp.sum(buf[...], axis=0)
 
     lane_sum = lambda x: jnp.sum(x, axis=1, keepdims=True)
@@ -298,35 +320,49 @@
     pl.semaphore_wait(known.at[1], nx - 1)
     ar_start(aa, 0, pack32(d0))
 
-    def halos(n):
-        for side in range(2):
-            @pl.when(z_from[side])
-            def _():
-                for y in range(ly):
-                    z_copy(n, side, y).wait_recv()
-            pl.when(y_from[side])(lambda: y_copy(n, side).wait_recv())
-
-    def local_rows(n, field, off, edges):
-        for y in order:
-            plus, minus = edges(y)
-            for j in range(nb):
-                v = field(off + y, j)
-                zp[y, 0, j * 8:(j + 1) * 8] = jnp.where(
-                    lane == lz - 1, pltpu.roll(plus, lz - 2 - 2 * j, 1), pltpu.roll(v, lz - 1, 1))
-                zp[y, 1, j * 8:(j + 1) * 8] = jnp.where(
-                    lane == 0, pltpu.roll(minus, lz - 2 * j, 1) if j else minus, pltpu.roll(v, 1, 1))
-        for y in order:
-            def body(j, acc):
-                at = pl.ds(pl.multiple_of(j * 8, 8), 8)
-                values = [field(off + y, j), field(off + y + 1, j), field(off + y - 1, j), zp[y, 0, at, :], zp[y, 1, at, :]]
-                acc = list(acc)
-                for k, v in zip(terms, values):
-                    for i in range(nb):
-                        acc[i] = acc[i] + spread(cf, (k, i), j * ly + y) * v
-                return tuple(acc)
-            acc = lax.fori_loop(0, nb, body, tuple(empty() for _ in range(nb)))
-            for i in range(nb):
-                loc[y, i * 8:(i + 1) * 8] = acc[i]
+    def own_row(field, y):
+        def body(j, acc):
+            at = pl.ds(pl.multiple_of(j * 8, 8), 8)
+            values = [(0, field(y, at)), (5, zp[y, 0, at, :]), (6, zp[y, 1, at, :])]
+            if y < ly - 1:
+                values.append((3, field(y + 1, at)))
+            if y > 0:
+                values.append((4, field(y - 1, at)))
+            acc = list(acc)
+            for k, v in values:
+                for i in range(nb):
+                    acc[i] = acc[i] + spread(cf, (k, i), j * ly + y) * v
+            return tuple(acc)
+        acc = lax.fori_loop(0, nb, body, tuple(empty() for _ in range(nb)))
+        for i in range(nb):
+            loc[y, i * 8:(i + 1) * 8] = acc[i]
+
+    def edge_row(n, y, plus, minus, field):
+        edge = jnp.where(lane % 2 == 1, plus, pltpu.roll(minus, 2, 1))
+        for j in range(nb):
+            hz[j * 8:(j + 1) * 8] = pltpu.roll(edge, lz - 2 - 2 * j, 1)
+
+        def body(j, acc):
+            at = pl.ds(pl.multiple_of(j * 8, 8), 8)
+            values = [(cz, (), hz[at, :])]
+            if y == ly - 1:
+                values.append((cf, (3,), field(ly, at)))
+            if y == 0:
+                values.append((cf, (4,), field(-1, at)))
+            acc = list(acc)
+            for ref, index, v in values:
+                for i in range(nb):
+                    acc[i] = acc[i] + spread(ref, index + (i,), j * ly + y) * v
+            return tuple(acc)
+        acc = pairs(body, tuple(loc[y, i * 8:(i + 1) * 8] for i in range(nb)))
+        for i in range(nb):
+            loc[y, i * 8:(i + 1) * 8] = acc[i]
+
+    def y_arrived(n, y):
+        if y == 0:
+            pl.when(y_from[0])(lambda: y_copy(n, 0).wait_recv())
+        if y == ly - 1:
+            pl.when(y_from[1])(lambda: y_copy(n, 1).wait_recv())
 
     def x_terms(n, y, value):
         acc = tuple(loc[y, i * 8:(i + 1) * 8] for i in range(nb))
@@ -337,19 +373,30 @@
             def body(j, acc):
                 v = value(side, y, pl.ds(pl.multiple_of(j * 8, 8), 8))
                 return tuple(acc[i] + spread(cf, (k, i), j * ly + y) * v for i in range(nb))
-            acc = lax.fori_loop(0, nb, body, acc)
+            acc = pairs(body, acc)
         return acc
 
+    def rows_of(ref):
+        return lambda y, at: ref[1 + y, at, :]
+
+    for y in order:
+        own_row(rows_of(vp.at[0]), y)
     for n in range(ITERS - 1):
-        halos(n)
-        local_rows(n, lambda y, j: vp[n, y, pl.ds(pl.multiple_of(j * 8, 8), 8), :], 1,
-                   lambda y: (zr[n, 0, y], zr[n, 1, y]))
         for y in order:
+            z_arrived(n, y)
+            y_arrived(n, y)
+            edge_row(n, y, zr[n, y, 0], zr[n, y, 1], rows_of(vp.at[n]))
             acc = x_terms(n, y, lambda side, y, at: xb[n, side, y, at, :])
             for i in range(nb):
                 vp[n + 1, 1 + y, i * 8:(i + 1) * 8] = acc[i]
             send_x(n + 1, y)
             send_yz(n + 1, y)
+            if n + 1 < ITERS - 1:
+                for i in range(nb):
+                    shifted(i, y, acc[i])
+        if n + 1 < ITERS - 1:
+            for y in order:
+                own_row(rows_of(vp.at[n + 1]), y)
 
     sums = ar_done(aa, 0)
     red0 = unpack32(sums[0:1], sums[1:2])
@@ -369,6 +416,8 @@
     for y in range(ly):
         p1[y] = shift1(vp[0, 1 + y], vp[1, 1 + y])
         p2[1 + y] = shift2(vp[0, 1 + y], vp[1, 1 + y], vp[2, 1 + y])
+        for j in range(nb):
+            shifted(j, y, p2[1 + y, j * 8:(j + 1) * 8])
     g1 = gram_end(gram(1), 16)
     g2 = gram_end(gram(2), 32)
     ar_start(ab, 1, pack32(g2) + pack16(g1) + [jnp.zeros((1, 128), F32)])
@@ -376,13 +425,16 @@
     for side in range(len(x_sides)):
         for y in range(ly):
             xg[side, y] = sig1 * xb[1, side, y] * inv1 + sig1 * shift1(xb[0, side, y], xb[1, side, y])
-    halos(2)
-    for h in (0, ly + 1):
-        p2[h] = shift2(vp[0, h], vp[1, h], vp[2, h])
-    local_rows(2, lambda y, j: p2[y, pl.ds(pl.multiple_of(j * 8, 8), 8), :], 1,
-               lambda y: tuple(shift2(zr[0, s, y], zr[1, s, y], zr[2, s, y]) for s in range(2)))
+    for y in order:
+        own_row(rows_of(p2), y)
     acc3 = gram_zero(3)
     for y in order:
+        z_arrived(2, y)
+        y_arrived(2, y)
+        for h, near in ((0, 0), (ly + 1, ly - 1)):
+            if y == near:
+                p2[h] = shift2(vp[0, h], vp[1, h], vp[2, h])
+        edge_row(2, y, *(shift2(zr[0, y, s], zr[1, y, s], zr[2, y, s]) for s in range(2)), rows_of(p2))
         acc = x_terms(2, y, lambda side, y, at: (xb[2, side, y, at, :] * inv1 - xg[side, y, at, :]) * inv1)
         for i in range(nb):
             p3[y, i * 8:(i + 1) * 8] = (acc[i] - sig1 * p2[1 + y, i * 8:(i + 1) * 8]) * inv1
@@ -398,13 +450,15 @@
         if n:
             rt = dot_nt(d, pad_rows(weights))
             s = pltpu.roll(d, 128 - base, 1) - dot_nt(rt, pad_rows([rt]))
-            low, aug = cholesky(s, unit - rt, base, row, lane)
+            lower, aug = cholesky(s, unit - rt, row, lane)
             weights.append(dot_nn(aug, pad_rows(weights + [unit])))
-            factors.append(rt + low)
         else:
-            low, aug = cholesky(d, unit, base, row, lane)
+            rt = empty()
+            lower, aug = cholesky(d, unit, row, lane)
             weights.append(aug)
-            factors.append(low)
+        for k in range(8):
+            rt = rt + jnp.where(lane == base + k, lower[k], 0.0)
+        factors.append(rt)
 
     def emit(n):
         cols = [column(weights[n], c) for c in range(8 * (n + 1))]
@@ -430,40 +484,55 @@
     factor(2, unpack32(sums[0:1], sums[1:2]))
     emit(2)
 
+    h = dot_nn(jnp.concatenate(weights + [empty()], axis=0), pad_rows(factors[1:]))
+    hr = lax.broadcasted_iota(jnp.int32, (32, 128), 0)
+    hl = lax.broadcasted_iota(jnp.int32, (32, 128), 1)
+    h = h * nu[0:1] + jnp.where(hr == hl, sigma[0:1], 0.0)
+    turned = jnp.concatenate([h, weights[2] * nu] + [empty()] * 11, axis=0).T
     small[8:32] = jnp.concatenate(weights, axis=0)
-    small[32:40] = factors[1]
-    small[40:48] = factors[2]
-    small[48:56] = sigma
-    small[56:64] = nu
-    for n in range(ITERS):
-        for side, entry in enumerate(x_sides):
-            def sent():
-                for y in range(ly):
-                    x_copy(n, side, y).wait_send()
-            when(entry[1], sent)
-        for side in range(2):
-            @pl.when(z_to[side])
-            def _():
-                for y in range(ly):
-                    z_copy(n, side, y).wait_send()
-            pl.when(y_to[side])(lambda: y_copy(n, side).wait_send())
+    small[32:40] = pltpu.roll(turned[16:24], 96, 1)
+    for i in range(ITERS + 1):
+        for j in range(ITERS):
+            block = turned[8 * i:8 * i + 8]
+            at = 8 * (i * ITERS + j) + 40
+            small[at:at + 8] = pltpu.roll(block, 128 - 8 * j, 1) if j else block
+    for side, entry in enumerate(x_sides):
+        when(entry[1], lambda: take(vp.at[:, 1:1 + ly], x_send.at[side]))
+    for side in range(2):
+        pl.when(z_to[side])(lambda: take(zs, z_send.at[side]))
+        pl.when(y_to[side])(lambda: take(vp.at[:, 0], y_send.at[side]))
     for m, buf in enumerate((aa, ab, ac)):
-        ar_wait(buf, a_send.at[m])
+        take(buf.at[0:ndev - 1], a_send.at[m])
     sums = ar_done(ac, 2)
     small[0:8] = unpack32(sums[0:1], sums[1:2])
 
 
-def finish(nb, nr, ly, q_ref, p3, small, basis_hbm, hess_hbm, rest, ob, hs, sem, hsem):
+def finish(nb, nr, ly, q_ref, p3, small, basis_hbm, hess_hbm, rest, ob, hs, sem):
     row, lane = tile_iota()
-    early = [pltpu.make_async_copy(q_ref.at[n], basis_hbm.at[n], sem.at[n]) for n in range(ITERS)]
-    for copy in early:
-        copy.start()
+    for n in range(ITERS):
+        pltpu.make_async_copy(q_ref.at[n], basis_hbm.at[n], sem.at[0]).start()
     base = 8 * ITERS
     d = jnp.where(lane < base + 8, small[0:8], 0.0)
-    weights = [small[8 * (n + 1):8 * (n + 2)] for n in range(ITERS)]
-    rt = dot_nt(d, pad_rows(weights))
+    rt = dot_nt(d, pad_rows([small[8 * (n + 1):8 * (n + 2)] for n in range(ITERS)]))
     s = pltpu.roll(d, 128 - base, 1) - dot_nt(rt, pad_rows([rt]))
     cols = [column(rt, c) for c in range(base)]
+    w2 = small[32:40]
+
+    def hess_block(i, j):
+        at = 8 * (i * ITERS + j) + 40
+        return small[at:at + 8]
+
+    def last(i, columns):
+        out = hess_block(i, ITERS - 1)
+        for r in range(8):
+            out = out + jnp.where(row == r, jnp.sum(columns[r] * w2, axis=0, keepdims=True), 0.0)
+        hs[i, ITERS - 1] = out[:, :8]
+
+    for i in range(ITERS + 1):
+        for j in range(ITERS - 1):
+            hs[i, j] = hess_block(i, j)[:, :8]
+    for i in range(ITERS):
+        last(i, cols[8 * i:8 * i + 8])
     for a in range(nb):
         for y in range(ly):
             parts = [p3[y, a * 8:(a + 1) * 8]]
@@ -475,9 +544,10 @@
                 parts.append(part)
             rest[y, a * 8:(a + 1) * 8] = parts[0] - ((parts[1] + parts[2]) + parts[3])
     unit = jnp.where(lane == row, 1.0, 0.0).astype(F32)
-    low, inverse = cholesky(s, unit, base, row, lane)
+    lower, inverse = cholesky(s, unit, row, lane)
+    last(ITERS, lower)
+    pltpu.make_async_copy(hs, hess_hbm, sem.at[1]).start()
     cols = [column(inverse, c) for c in range(8)]
-    late = []
     half = nb // 2
     for h in range(2):
         for a in range(h * half, (h + 1) * half):
@@ -486,22 +556,9 @@
                 total = ((part[0] + part[1]) + (part[2] + part[3])) + ((part[4] + part[5]) + (part[6] + part[7]))
                 ob[pl.ds(a * nr * ly + y, 8, stride=ly), :] = total
         at = pl.ds(h * half * nr * ly, half * nr * ly)
-        copy = pltpu.make_async_copy(ob.at[at], basis_hbm.at[ITERS, at], sem.at[ITERS + h])
-        copy.start()
-        late.append(copy)
-    factors = [small[32:40], small[40:48], rt + low]
-    h = dot_nn(jnp.concatenate(weights + [empty()], axis=0), pad_rows(factors))
-    hr = lax.broadcasted_iota(jnp.int32, (32, 128), 0)
-    hl = lax.broadcasted_iota(jnp.int32, (32, 128), 1)
-    h = h * small[56:57] + jnp.where(hr == hl, small[48:49], 0.0)
-    t = jnp.concatenate([h, jnp.zeros((96, 128), F32)], axis=0).T
-    for i in range(ITERS + 1):
-        for j in range(ITERS):
-            hs[i, j] = t[8 * i:8 * i + 8, 8 * j:8 * j + 8]
-    copy = pltpu.make_async_copy(hs, hess_hbm, hsem)
-    copy.start()
-    for c in early + late + [copy]:
-        c.wait()
+        pltpu.make_async_copy(ob.at[at], basis_hbm.at[ITERS, at], sem.at[0]).start()
+    pltpu.make_async_copy(basis_hbm, basis_hbm, sem.at[0]).wait()
+    pltpu.make_async_copy(hs, hess_hbm, sem.at[1]).wait()
 
 
 def shards(mesh_sizes, rhs, blocks):
@@ -521,7 +578,7 @@
         out_shape=(
             jax.ShapeDtypeStruct((ITERS, nb * nr * ly, lz), F32),
             jax.ShapeDtypeStruct((ly, nb * 8, lz), F32),
-            jax.ShapeDtypeStruct((64, lz), F32),
+            jax.ShapeDtypeStruct((40 + 8 * ITERS * (ITERS + 1), lz), F32),
         ),
         in_specs=[hbm] * 2,
         out_specs=(vmem,) * 3,
@@ -529,21 +586,23 @@
             vm(nb * nr * ly, lz),
             pltpu.VMEM((7, nb, nb * ly, lz), jnp.bfloat16),
             vm(7, nb, nb * ly, lz),
+            vm(nb, nb * ly, lz),
             vm(ITERS, ly + 2, nb * 8, lz),
             vm(ly, nb * 8, lz),
             vm(ly + 2, nb * 8, lz),
             vm(ITERS, sides, ly, nb * 8, lz),
             vm(sides, ly, nb * 8, lz),
             vm(ITERS, ly, 8, lz),
-            vm(ITERS, 2, ly, 8, lz),
+            vm(ITERS, ly, 2, 8, lz),
             vm(ly, 2, nb * 8, lz),
+            vm(nb * 8, lz),
             vm(ly, nb * 8, lz),
             vm(ndev, 2, lz), vm(ndev, 4, lz), vm(ndev, 2, lz),
-            dma((ITERS, sides, ly)), dma((ITERS, sides, ly)),
-            dma((ITERS, 2)), dma((ITERS, 2)),
-            dma((ITERS, 2, ly)), dma((ITERS, 2, ly)),
+            dma((sides,)), dma((2, sides, ly)),
+            dma((2,)), dma((2, 2)),
+            dma((2,)), dma((2, ly)),
             dma((3,)), dma((3,)),
-            dma((8,)),
+            dma((2,)),
             pltpu.SemaphoreType.REGULAR((2,)),
         ],
         compiler_params=pltpu.CompilerParams(collective_id=0, has_side_effects=True, vmem_limit_bytes=48 * 1024 * 1024),
@@ -560,8 +619,7 @@
             vm(ly, nb * 8, lz),
             vm(nb * nr * ly, lz),
             vm(ITERS + 1, ITERS, 8, 8),
-            dma((ITERS + 2,)),
-            dma,
+            dma((2,)),
         ],
         compiler_params=pltpu.CompilerParams(vmem_limit_bytes=8 * 1024 * 1024),
     )(q, p3, small)

time: 27.6 us -> 24.7 us (0.89)
  Pallas kernels: 26.8 us -> 23.9 us
    pallas_call x1, Pallas kernels: 25.4 us -> 22.6 us  [shards(): pl.pallas_call(functools.partial(krylov, mesh_sizes, nb, nr, ly, lz), out...]
where the time goes in v2:
time: 24.7 us; the launch traced here: 24.6 us
  Pallas kernels  23.9 us (97%)
  between operations  0.64 us (3%)
    pallas_call x1, Pallas kernels, shards(): pl.pallas_call(functools.partial(krylov, mesh_sizes, nb, nr, ly, lz), out...  22.6 us
    pallas_call x1, Pallas kernels, shards(): pl.pallas_call(functools.partial(finish, nb, nr, ly), out_shape=(jax.Shap...  1.35 us

profile of v2, /device:TPU:0, one launch (start us, length us, event | category | flops | bytes accessed | tf_op | source)
XLA Modules:
  0.0 24.6 jit_solution(1261865129441021991)
XLA Ops:
  0.6 22.6 %shard_map.41 = (f32[3,256,128]{2,1,0:T(8,128)S(1)}, f32[4,64,128]{2,1,0:T(8,128)S(1)}, f32[136,128]{1,0:T(8,128)S(1)}) custom-call(f32[256,128]{1,0:T(8,128)} %bitcast.7, bf16[7,8,32,128]{3,2,1,0:T(8,128)(2,1)} %bitcast.6), custom_call_target="tpu_custom_call" | custom-call | tf_op jit(solution)/shard_map/pallas_call | solution.py:576
  23.2 1.3 %shard_map.42 = (f32[4,256,128]{2,1,0:T(8,128)}, f32[4,3,8,8]{3,2,1,0:T(8,128)}) custom-call(f32[3,256,128]{2,1,0:T(8,128)S(1)} %get-tuple-element.7.q_ref, f32[4,64,128]{2,1,0:T(8,128)S(1)} %get-tuple-element.8.p3, f32[136,128]{1,0:T(8,128)S(1)} %get-tuple-element.9.small), custom_call_target="tpu_custom_call" | custom-call | tf_op jit(solution)/shard_map/pallas_call | solution.py:610

commit v3 on v2

--- a/solution.py
+++ b/solution.py
@@ -14,10 +14,6 @@
 MESH = pl.DeviceIdType.MESH
 
 
-def dot_nt(a, b):
-    return lax.dot_general(a, b, (((1,), (1,)), ((), ())), precision=HIGH, preferred_element_type=F32)
-
-
 def dot_nn(a, b):
     return lax.dot_general(a, b, (((1,), (0,)), ((), ())), precision=HIGH, preferred_element_type=F32)
 
@@ -44,26 +40,51 @@
     return jnp.broadcast_to(m[:, c:c + 1], (8, 128))
 
 
-def cholesky(s, aug, row, lane):
-    cols = [column(s, c) for c in range(8)]
+def sub(v, r):
+    return jnp.broadcast_to(v[r:r + 1], (8, 128))
+
+
+def root(v, r):
+    piv = sub(v, r)
+    rs = lax.rsqrt(piv)
+    return rs * (1.5 - 0.5 * piv * rs * rs)
+
+
+def tree(parts):
+    while len(parts) > 1:
+        parts = [a + b for a, b in zip(parts[::2], parts[1::2])] + parts[len(parts) // 2 * 2:]
+    return parts[0]
+
+
+def cholesky(tiles, rhs, row):
+    count = len(tiles)
+    rhs = [list(r) for r in rhs]
+    cols = [{b: tiles[b](c) for b in range(c // 8, count)} for c in range(8 * count)]
     lower = []
-    for k in range(8):
-        piv = jnp.broadcast_to(cols[k][k:k + 1], (8, 128))
-        rs = lax.rsqrt(piv)
-        rs = rs * (1.5 - 0.5 * piv * rs * rs)
-        lk = jnp.where(row >= k, cols[k] * rs, 0.0)
+    for k in range(8 * count):
+        kb, kr = divmod(k, 8)
+        rs = root(cols[k][kb], kr)
+        lk = {b: cols[k][b] * rs for b in range(kb, count)}
+        lk[kb] = jnp.where(row >= kr, lk[kb], 0.0)
         lower.append(lk)
-        arow = jnp.broadcast_to(aug[k:k + 1], (8, 128)) * rs
-        aug = jnp.where(row == k, arow, aug - jnp.where(row > k, lk, 0.0) * arow)
-        for c in range(k + 1, 8):
-            cols[c] = cols[c] - lk * jnp.broadcast_to(lk[c:c + 1], (8, 128))
-    return lower, aug
+        under = jnp.where(row > kr, lk[kb], 0.0)
+        for t in range(len(rhs[0])):
+            arow = sub(rhs[kb][t], kr) * rs
+            rhs[kb][t] = jnp.where(row == kr, arow, rhs[kb][t] - under * arow)
+            for b in range(kb + 1, count):
+                rhs[b][t] = rhs[b][t] - lk[b] * arow
+        for c in range(k + 1, 8 * count):
+            cb, cr = divmod(c, 8)
+            f = sub(lk[cb], cr)
+            for b in range(cb, count):
+                cols[c][b] = cols[c][b] - lk[b] * f
+    return lower, rhs
 
 
 def krylov(
     mesh_sizes, nb, nr, ly, lz,
     rhs_hbm, blk_hbm, q_ref, p3, small,
-    rv, bv, cf, cz, vp, p1, p2, xb, xg, zs, zr, zp, hz, loc, aa, ab, ac,
+    rv, bv, cf, cz, vp, p1, p2, xb, xg, zs, zr, zp, hz, loc, aa, rbc,
     x_send, x_recv, y_send, y_recv, z_send, z_recv, a_send, a_recv, in_sem, known,
 ):
     nx, ny, nz = mesh_sizes
@@ -94,9 +115,6 @@
                 return c
             lax.fori_loop(1, size, body, 0)
 
-    for axis in AXES[::-1]:
-        greet(barrier, axis)
-
     if nx == 1:
         x_sides = []
     elif nx == 2:
@@ -110,6 +128,24 @@
         else:
             pl.when(cond)(fn)
 
+    places = {"gx": (nx, gx), "gy": (ny, gy), "gz": (nz, gz)}
+
+    def near(sem, axes):
+        for axis in axes:
+            size, at = places[axis]
+            for cond, target in ((at > 0, at - 1), (at < size - 1, at + 1)):
+                if size > 1:
+                    pl.when(cond)(lambda: pl.semaphore_signal(
+                        sem, inc=1, device_id={axis: target}, device_id_type=MESH))
+
+    def near_wait(sem, axes):
+        pl.semaphore_wait(sem, sum(jnp.minimum(places[a][1], 1) + jnp.minimum(places[a][0] - 1 - places[a][1], 1)
+                                   for a in axes if places[a][0] > 1))
+
+    near(barrier, AXES[::-1])
+    wave_axes = [a for a in AXES[::-1] if places[a][0] > 2]
+    waves = max(nx, ny, nz) - 2 if wave_axes else 0
+
     def remote(src, dst, ssem, rsem, dev):
         return pltpu.make_async_remote_copy(
             src_ref=src, dst_ref=dst, send_sem=ssem, recv_sem=rsem, device_id=dev, device_id_type=MESH)
@@ -126,11 +162,11 @@
     def y_copy(n, side):
         if side == 0:
             return remote(vp.at[n, ly], vp.at[n, 0], y_send.at[0], y_recv.at[n % 2, 0], {"gy": gy + 1})
-        return remote(vp.at[n, 1], vp.at[n, ly + 1], y_send.at[1], y_recv.at[n % 2, 1], {"gy": gy - 1})
+        return remote(vp.at[n, 1], vp.at[n, ly + 1], y_send.at[0], y_recv.at[n % 2, 1], {"gy": gy - 1})
 
     def z_copy(n, side, y):
         target = gz - 1 if side == 0 else gz + 1
-        return remote(zs.at[n, y], zr.at[n, y, side], z_send.at[side], z_recv.at[n % 2, y], {"gz": target})
+        return remote(zs.at[n, y], zr.at[n, y, side], z_send.at[0], z_recv.at[n % 2, y], {"gz": target})
 
     def take(ref, sem):
         pltpu.make_async_copy(ref, ref, sem).wait()
@@ -186,10 +222,11 @@
     for y in order:
         for a in range(nb):
             vp[0, 1 + y, a * 8:(a + 1) * 8] = rv[pl.ds(a * nr * ly + y, 8, stride=ly), :]
-    pl.semaphore_wait(barrier, nx + ny + nz - 3)
+    near_wait(barrier, AXES)
     for y in order:
         send_x(0, y)
-    greet(known.at[0], "gy")
+    if waves:
+        near(known.at[0], wave_axes)
     for y in order:
         send_yz(0, y)
 
@@ -230,29 +267,32 @@
         return lax.fori_loop(0, nb // 2, lambda t, acc: body(2 * t + 1, body(2 * t, acc)), acc)
 
     views = [(vp, (0,), 1), (p1, (), 0), (p2, (), 1), (p3, (), 0)]
-
-    def tile(i, y, a):
-        ref, index, off = views[i]
+    raw = [(vp, (0,), 1), (vp, (1,), 1)]
+
+    def tile(i, y, a, fields):
+        ref, index, off = fields[i]
         return ref[index + (off + y, pl.ds(pl.multiple_of(a * 8, 8), 8), slice(None))]
 
-    def tile_row(i, y, r):
-        ref, index, off = views[i]
+    def tile_row(i, y, r, fields):
+        ref, index, off = fields[i]
         return spread(ref, index + (off + y,), r)
 
     def gram_row(n, y, acc):
+        own = raw if n < 2 else views
+
         def body(a, acc):
-            p = tile(n, y, a)
-            return tuple(acc[i * 8 + s] + p * tile_row(i, y, a * 8 + s)
+            p = tile(n, y, a, own)
+            return tuple(acc[i * 8 + s] + p * tile_row(i, y, a * 8 + s, own)
                          for i in range(n + 1) for s in range(8))
         return pairs(body, acc)
 
     def gram_zero(n):
         return tuple(empty() for _ in range(8 * (n + 1)))
 
-    def gram_end(acc, width):
+    def gram_end(acc, first=0):
         d = empty()
         for k, part in enumerate(acc):
-            d = jnp.where(lane % width == k, jnp.sum(part, axis=1, keepdims=True), d)
+            d = jnp.where(lane % 32 == first + k, jnp.sum(part, axis=1, keepdims=True), d)
         return d
 
     def gram(n):
@@ -265,22 +305,11 @@
         d = jnp.where(lane // 32 == row % 4, d, 0.0)
         return [jnp.sum(d[0:4], axis=0, keepdims=True), jnp.sum(d[4:8], axis=0, keepdims=True)]
 
-    def pack16(d):
-        d = jnp.where(lane // 16 == row, d, 0.0)
-        return [jnp.sum(d, axis=0, keepdims=True)]
-
-    def unpack32(t0, t1):
-        z = jnp.where(row < 4, t0, t1)
+    def unpack32(sums):
+        z = jnp.where(row < 4, sums[0:1], sums[1:2])
         out = z
         for g in range(1, 4):
             out = jnp.where(row % 4 == g, pltpu.roll(z, 128 - 32 * g, 1), out)
-        return out
-
-    def unpack16(t):
-        z = jnp.broadcast_to(t, (8, 128))
-        out = z
-        for g in range(1, 8):
-            out = jnp.where(row == g, pltpu.roll(z, 128 - 16 * g, 1), out)
         return out
 
     def ends(at, size):
@@ -295,13 +324,13 @@
             for z in ends(gz, nz):
                 for dx in range(nx):
                     for dy in range(ny):
-                        copy = remote(buf.at[me], buf.at[me], a_send.at[m], a_recv.at[m], (xs[dx], ys[dy], z))
+                        copy = remote(buf.at[me], buf.at[me], a_send.at[min(m, 1)], a_recv.at[m], (xs[dx], ys[dy], z))
                         own = dx == nx - 1 and (dy + ny // 2) % ny == 0
                         when(z != gz if own else None, copy.start)
         else:
             def body(d, c):
                 t = lax.rem(me + d, ndev)
-                remote(buf.at[me], buf.at[me], a_send.at[m], a_recv.at[m],
+                remote(buf.at[me], buf.at[me], a_send.at[min(m, 1)], a_recv.at[m],
                        (t // (ny * nz), (t // nz) % ny, t % nz)).start()
                 return c
             lax.fori_loop(1, ndev, body, 0)
@@ -311,14 +340,6 @@
         return jnp.sum(buf[...], axis=0)
 
     lane_sum = lambda x: jnp.sum(x, axis=1, keepdims=True)
-    pl.semaphore_wait(known.at[0], ny - 1)
-    greet(known.at[1], "gx")
-    d0 = gram_end(gram(0), 32)
-    d0 = d0 + jnp.where(lane % 32 == 8, jnp.where(row < ly, lane_sum(jnp.concatenate(
-        [trace, jnp.zeros((8 - ly, 128), F32)], axis=0)), 0.0), 0.0)
-    d0 = d0 + jnp.where(lane % 32 == 9, lane_sum(total_abs), 0.0)
-    pl.semaphore_wait(known.at[1], nx - 1)
-    ar_start(aa, 0, pack32(d0))
 
     def own_row(field, y):
         def body(j, acc):
@@ -333,14 +354,14 @@
                 for i in range(nb):
                     acc[i] = acc[i] + spread(cf, (k, i), j * ly + y) * v
             return tuple(acc)
-        acc = lax.fori_loop(0, nb, body, tuple(empty() for _ in range(nb)))
+        acc = pairs(body, tuple(empty() for _ in range(nb)))
         for i in range(nb):
             loc[y, i * 8:(i + 1) * 8] = acc[i]
 
     def edge_row(n, y, plus, minus, field):
-        edge = jnp.where(lane % 2 == 1, plus, pltpu.roll(minus, 2, 1))
         for j in range(nb):
-            hz[j * 8:(j + 1) * 8] = pltpu.roll(edge, lz - 2 - 2 * j, 1)
+            first = pltpu.roll(minus, lz - 2 * j, 1) if j else minus
+            hz[j * 8:(j + 1) * 8] = jnp.where(lane == 0, first, pltpu.roll(plus, lz - 2 - 2 * j, 1))
 
         def body(j, acc):
             at = pl.ds(pl.multiple_of(j * 8, 8), 8)
@@ -379,10 +400,37 @@
     def rows_of(ref):
         return lambda y, at: ref[1 + y, at, :]
 
+    def shift1(v0, v1):
+        return (v1 - sig1 * v0) * inv1
+
+    def shift2(v0, v1, v2):
+        return ((v2 - sig1 * v1) * inv1 - sig1 * shift1(v0, v1)) * inv1
+
+    for w in range(1, waves):
+        near_wait(known.at[(w - 1) % 2], wave_axes)
+        near(known.at[w % 2], wave_axes)
     for y in order:
         own_row(rows_of(vp.at[0]), y)
+    if waves:
+        near_wait(known.at[(waves - 1) % 2], wave_axes)
+    greet(known.at[2], "gy")
+    h00 = gram_end(gram(0), 16)
+    traces = lane_sum(jnp.sum(trace, axis=0, keepdims=True))
+    sizes = lane_sum(jnp.sum(total_abs, axis=0, keepdims=True))
+    totals = jnp.where(lane[0:1] == 0, traces, jnp.where(lane[0:1] == 1, sizes, 0.0))
+
+    def presence(step):
+        if step == min(1, ly - 1):
+            pl.semaphore_wait(known.at[2], ny - 1)
+            greet(known.at[3], "gx")
+        if step == ly - 1:
+            pl.semaphore_wait(known.at[3], nx - 1)
+            ar_start(aa, 0, [totals])
+
     for n in range(ITERS - 1):
-        for y in order:
+        for step, y in enumerate(order):
+            if n == 0:
+                presence(step)
             z_arrived(n, y)
             y_arrived(n, y)
             edge_row(n, y, zr[n, y, 0], zr[n, y, 1], rows_of(vp.at[n]))
@@ -397,30 +445,21 @@
         if n + 1 < ITERS - 1:
             for y in order:
                 own_row(rows_of(vp.at[n + 1]), y)
+            ar_start(rbc.at[0], 1, pack32(gram_end(gram(1)) + h00))
 
     sums = ar_done(aa, 0)
-    red0 = unpack32(sums[0:1], sums[1:2])
-    sigma = jnp.broadcast_to(lane_sum(jnp.where((row < ly) & (lane == 8), red0, 0.0)), (8, 128))
-    sigma = jnp.broadcast_to(jnp.sum(sigma, axis=0, keepdims=True), (8, 128)) / (8.0 * cells)
-    nu = jnp.broadcast_to(lane_sum(jnp.where(lane == 9, red0, 0.0)), (8, 128))
-    nu = jnp.broadcast_to(jnp.sum(nu, axis=0, keepdims=True), (8, 128)) / (8.0 * cells)
-    inv = 1.0 / nu
-    sig1, inv1 = sigma[0:1], inv[0:1]
-
-    def shift1(v0, v1):
-        return (v1 - sig1 * v0) * inv1
-
-    def shift2(v0, v1, v2):
-        return ((v2 - sig1 * v1) * inv1 - sig1 * shift1(v0, v1)) * inv1
-
+    sig1 = jnp.broadcast_to(sums[:, 0:1] / (8.0 * cells), (1, 128))
+    nu1 = jnp.broadcast_to(sums[:, 1:2] / (8.0 * cells), (1, 128))
+    inv1 = 1.0 / nu1
     for y in range(ly):
         p1[y] = shift1(vp[0, 1 + y], vp[1, 1 + y])
+
+    for y in range(ly):
         p2[1 + y] = shift2(vp[0, 1 + y], vp[1, 1 + y], vp[2, 1 + y])
         for j in range(nb):
             shifted(j, y, p2[1 + y, j * 8:(j + 1) * 8])
-    g1 = gram_end(gram(1), 16)
-    g2 = gram_end(gram(2), 32)
-    ar_start(ab, 1, pack32(g2) + pack16(g1) + [jnp.zeros((1, 128), F32)])
+    g2 = gram_end(gram(2))
+    ar_start(rbc.at[1], 2, pack32(g2))
 
     for side in range(len(x_sides)):
         for y in range(ly):
@@ -439,57 +478,42 @@
         for i in range(nb):
             p3[y, i * 8:(i + 1) * 8] = (acc[i] - sig1 * p2[1 + y, i * 8:(i + 1) * 8]) * inv1
         acc3 = gram_row(3, y, acc3)
-    ar_start(ac, 2, pack32(gram_end(acc3, 32)))
-
-    weights, factors = [], []
-
-    def factor(n, red):
-        base = 8 * n
-        unit = jnp.where(lane == base + row, 1.0, 0.0).astype(F32)
-        d = jnp.where(lane < base + 8, red, 0.0)
-        if n:
-            rt = dot_nt(d, pad_rows(weights))
-            s = pltpu.roll(d, 128 - base, 1) - dot_nt(rt, pad_rows([rt]))
-            lower, aug = cholesky(s, unit - rt, row, lane)
-            weights.append(dot_nn(aug, pad_rows(weights + [unit])))
-        else:
-            rt = empty()
-            lower, aug = cholesky(d, unit, row, lane)
-            weights.append(aug)
-        for k in range(8):
-            rt = rt + jnp.where(lane == base + k, lower[k], 0.0)
-        factors.append(rt)
+    ar_start(rbc.at[2], 3, pack32(gram_end(acc3)))
 
     def emit(n):
         cols = [column(weights[n], c) for c in range(8 * (n + 1))]
 
-        def body(a, c):
+        for a in range(nb):
             for y in range(ly):
                 parts = []
                 for i in range(n + 1):
                     part = None
                     for s in range(8):
-                        t = cols[i * 8 + s] * tile_row(i, y, a * 8 + s)
+                        t = cols[i * 8 + s] * tile_row(i, y, a * 8 + s, views)
                         part = t if part is None else part + t
                     parts.append(part)
                 q_ref[n, pl.ds(a * nr * ly + y, 8, stride=ly), :] = sum(parts[1:], parts[0])
-            return c
-        lax.fori_loop(0, nb, body, 0)
-
-    factor(0, red0)
-    emit(0)
-    sums = ar_done(ab, 1)
-    factor(1, unpack16(sums[2:3]))
-    emit(1)
-    factor(2, unpack32(sums[0:1], sums[1:2]))
-    emit(2)
+
+    h = unpack32(ar_done(rbc.at[0], 1))
+    turn = jnp.concatenate([h] + [empty()] * 15, axis=0).T[0:8]
+    both = pltpu.roll(h, 8, 1) + pltpu.roll(turn, 8, 1)
+    first = pltpu.roll(h, 112, 1)
+    g1 = jnp.where(lane < 8, (h - sig1 * first) * inv1,
+                   ((h - sig1 * both) + sig1 * sig1 * pltpu.roll(h, 120, 1)) * (inv1 * inv1))
+    grams = [first, g1, unpack32(ar_done(rbc.at[1], 2))]
+    units = [[jnp.where(lane == 8 * n + row, 1.0, 0.0).astype(F32)] for n in range(ITERS)]
+    lower, weights = cholesky([functools.partial(column, g) for g in grams], units, row)
+    weights = [w[0] for w in weights]
+    factors = [tree([jnp.where(lane == k, lower[k][n], 0.0) for k in range(8 * (n + 1))]) for n in range(ITERS)]
+    for n in range(ITERS):
+        emit(n)
 
     h = dot_nn(jnp.concatenate(weights + [empty()], axis=0), pad_rows(factors[1:]))
     hr = lax.broadcasted_iota(jnp.int32, (32, 128), 0)
     hl = lax.broadcasted_iota(jnp.int32, (32, 128), 1)
-    h = h * nu[0:1] + jnp.where(hr == hl, sigma[0:1], 0.0)
-    turned = jnp.concatenate([h, weights[2] * nu] + [empty()] * 11, axis=0).T
-    small[8:32] = jnp.concatenate(weights, axis=0)
+    h = h * nu1 + jnp.where(hr == hl, sig1, 0.0)
+    turned = jnp.concatenate([h, weights[2] * nu1] + [empty()] * 11, axis=0).T
+    small[8:32] = jnp.concatenate(weights + [empty()] * 13, axis=0).T[0:24]
     small[32:40] = pltpu.roll(turned[16:24], 96, 1)
     for i in range(ITERS + 1):
         for j in range(ITERS):
@@ -498,13 +522,12 @@
             small[at:at + 8] = pltpu.roll(block, 128 - 8 * j, 1) if j else block
     for side, entry in enumerate(x_sides):
         when(entry[1], lambda: take(vp.at[:, 1:1 + ly], x_send.at[side]))
-    for side in range(2):
-        pl.when(z_to[side])(lambda: take(zs, z_send.at[side]))
-        pl.when(y_to[side])(lambda: take(vp.at[:, 0], y_send.at[side]))
-    for m, buf in enumerate((aa, ab, ac)):
-        take(buf.at[0:ndev - 1], a_send.at[m])
-    sums = ar_done(ac, 2)
-    small[0:8] = unpack32(sums[0:1], sums[1:2])
+    for to, both_sides, one_side, sem in ((z_to, zr, zs, z_send), (y_to, vp.at[:, 0:2], vp.at[:, 0], y_send)):
+        pl.when(jnp.logical_and(to[0], to[1]))(lambda: take(both_sides, sem.at[0]))
+        pl.when(to[0] != to[1])(lambda: take(one_side, sem.at[0]))
+    take(aa.at[0:ndev - 1], a_send.at[0])
+    take(rbc.at[:, 0:ndev - 1], a_send.at[1])
+    small[0:8] = unpack32(ar_done(rbc.at[2], 3))
 
 
 def finish(nb, nr, ly, q_ref, p3, small, basis_hbm, hess_hbm, rest, ob, hs, sem):
@@ -512,9 +535,9 @@
     for n in range(ITERS):
         pltpu.make_async_copy(q_ref.at[n], basis_hbm.at[n], sem.at[0]).start()
     base = 8 * ITERS
-    d = jnp.where(lane < base + 8, small[0:8], 0.0)
-    rt = dot_nt(d, pad_rows([small[8 * (n + 1):8 * (n + 2)] for n in range(ITERS)]))
-    s = pltpu.roll(d, 128 - base, 1) - dot_nt(rt, pad_rows([rt]))
+    d = small[0:8]
+    dcols = [column(d, c) for c in range(base + 8)]
+    rt = tree([dcols[c] * spread(small, (), 8 + c) for c in range(base)])
     cols = [column(rt, c) for c in range(base)]
     w2 = small[32:40]
 
@@ -535,26 +558,23 @@
         last(i, cols[8 * i:8 * i + 8])
     for a in range(nb):
         for y in range(ly):
-            parts = [p3[y, a * 8:(a + 1) * 8]]
-            for i in range(ITERS):
-                part = None
-                for t in range(8):
-                    u = cols[i * 8 + t] * spread(q_ref, (i,), a * nr * ly + t * ly + y)
-                    part = u if part is None else part + u
-                parts.append(part)
-            rest[y, a * 8:(a + 1) * 8] = parts[0] - ((parts[1] + parts[2]) + parts[3])
+            parts = [cols[8 * i + t] * spread(q_ref, (i,), a * nr * ly + t * ly + y) for i in range(ITERS) for t in range(8)]
+            rest[y, a * 8:(a + 1) * 8] = p3[y, a * 8:(a + 1) * 8] - tree(parts)
+
+    def gram_column(c):
+        return dcols[base + c] - tree([cols[m] * sub(cols[m], c) for m in range(base)])
+
     unit = jnp.where(lane == row, 1.0, 0.0).astype(F32)
-    lower, inverse = cholesky(s, unit, row, lane)
-    last(ITERS, lower)
+    lower, inverse = cholesky([gram_column], [[unit]], row)
+    last(ITERS, [lk[0] for lk in lower])
     pltpu.make_async_copy(hs, hess_hbm, sem.at[1]).start()
-    cols = [column(inverse, c) for c in range(8)]
+    cols = [column(inverse[0][0], c) for c in range(8)]
     half = nb // 2
     for h in range(2):
         for a in range(h * half, (h + 1) * half):
             for y in range(ly):
-                part = [cols[t] * spread(rest, (y,), a * 8 + t) for t in range(8)]
-                total = ((part[0] + part[1]) + (part[2] + part[3])) + ((part[4] + part[5]) + (part[6] + part[7]))
-                ob[pl.ds(a * nr * ly + y, 8, stride=ly), :] = total
+                ob[pl.ds(a * nr * ly + y, 8, stride=ly), :] = tree(
+                    [cols[t] * spread(rest, (y,), a * 8 + t) for t in range(8)])
         at = pl.ds(h * half * nr * ly, half * nr * ly)
         pltpu.make_async_copy(ob.at[at], basis_hbm.at[ITERS, at], sem.at[0]).start()
     pltpu.make_async_copy(basis_hbm, basis_hbm, sem.at[0]).wait()
@@ -597,13 +617,13 @@
             vm(ly, 2, nb * 8, lz),
             vm(nb * 8, lz),
             vm(ly, nb * 8, lz),
-            vm(ndev, 2, lz), vm(ndev, 4, lz), vm(ndev, 2, lz),
+            vm(ndev, 1, lz), vm(3, ndev, 2, lz),
             dma((sides,)), dma((2, sides, ly)),
-            dma((2,)), dma((2, 2)),
-            dma((2,)), dma((2, ly)),
-            dma((3,)), dma((3,)),
+            dma((1,)), dma((2, 2)),
+            dma((1,)), dma((2, ly)),
+            dma((2,)), dma((4,)),
             dma((2,)),
-            pltpu.SemaphoreType.REGULAR((2,)),
+            pltpu.SemaphoreType.REGULAR((4,)),
         ],
         compiler_params=pltpu.CompilerParams(collective_id=0, has_side_effects=True, vmem_limit_bytes=48 * 1024 * 1024),
     )(rhs2, blk2)

time: 24.7 us -> 23.6 us (0.955)
  Pallas kernels: 23.9 us -> 22.8 us
    pallas_call x1, Pallas kernels: 22.6 us -> 21.5 us  [shards(): pl.pallas_call(functools.partial(krylov, mesh_sizes, nb, nr, ly, lz), out...]
where the time goes in v3:
time: 23.6 us; the launch traced here: 23.4 us
  Pallas kernels  22.8 us (97%)
  between operations  0.64 us (3%)
    pallas_call x1, Pallas kernels, shards(): pl.pallas_call(functools.partial(krylov, mesh_sizes, nb, nr, ly, lz), out...  21.5 us
    pallas_call x1, Pallas kernels, shards(): pl.pallas_call(functools.partial(finish, nb, nr, ly), out_shape=(jax.Shap...  1.32 us

profile of v3, /device:TPU:0, one launch (start us, length us, event | category | flops | bytes accessed | tf_op | source)
XLA Modules:
  0.0 23.4 jit_solution(5743619011845363094)
XLA Ops:
  0.6 21.5 %shard_map.41 = (f32[3,256,128]{2,1,0:T(8,128)S(1)}, f32[4,64,128]{2,1,0:T(8,128)S(1)}, f32[136,128]{1,0:T(8,128)S(1)}) custom-call(f32[256,128]{1,0:T(8,128)} %bitcast.7, bf16[7,8,32,128]{3,2,1,0:T(8,128)(2,1)} %bitcast.6), custom_call_target="tpu_custom_call" | custom-call | tf_op jit(solution)/shard_map/pallas_call | solution.py:596
  22.1 1.3 %shard_map.42 = (f32[4,256,128]{2,1,0:T(8,128)}, f32[4,3,8,8]{3,2,1,0:T(8,128)}) custom-call(f32[3,256,128]{2,1,0:T(8,128)S(1)} %get-tuple-element.7.q_ref, f32[4,64,128]{2,1,0:T(8,128)S(1)} %get-tuple-element.8.p3, f32[136,128]{1,0:T(8,128)S(1)} %get-tuple-element.9.small), custom_call_target="tpu_custom_call" | custom-call | tf_op jit(solution)/shard_map/pallas_call | solution.py:630

commit v4 on v3

--- a/solution.py
+++ b/solution.py
@@ -14,6 +14,10 @@
 MESH = pl.DeviceIdType.MESH
 
 
+def dot_nt(a, b):
+    return lax.dot_general(a, b, (((1,), (1,)), ((), ())), precision=HIGH, preferred_element_type=F32)
+
+
 def dot_nn(a, b):
     return lax.dot_general(a, b, (((1,), (0,)), ((), ())), precision=HIGH, preferred_element_type=F32)
 
@@ -56,35 +60,33 @@
     return parts[0]
 
 
-def cholesky(tiles, rhs, row):
-    count = len(tiles)
-    rhs = [list(r) for r in rhs]
-    cols = [{b: tiles[b](c) for b in range(c // 8, count)} for c in range(8 * count)]
-    lower = []
-    for k in range(8 * count):
+def factor_block(tile, rhs, lower, scale, solved, row):
+    b = len(solved)
+    size = 8 * (b + 1)
+    cols = [tile(c) for c in range(size)]
+    for k in range(size):
         kb, kr = divmod(k, 8)
-        rs = root(cols[k][kb], kr)
-        lk = {b: cols[k][b] * rs for b in range(kb, count)}
-        lk[kb] = jnp.where(row >= kr, lk[kb], 0.0)
-        lower.append(lk)
-        under = jnp.where(row > kr, lk[kb], 0.0)
-        for t in range(len(rhs[0])):
-            arow = sub(rhs[kb][t], kr) * rs
-            rhs[kb][t] = jnp.where(row == kr, arow, rhs[kb][t] - under * arow)
-            for b in range(kb + 1, count):
-                rhs[b][t] = rhs[b][t] - lk[b] * arow
-        for c in range(k + 1, 8 * count):
+        if kb < b:
+            lk = cols[k] * scale[k]
+            lower[k][b] = lk
+            rhs = rhs - lk * sub(solved[kb], kr)
+        else:
+            rs = root(cols[k], kr)
+            lk = jnp.where(row >= kr, cols[k] * rs, 0.0)
+            scale.append(rs)
+            lower.append({b: lk})
+            arow = sub(rhs, kr) * rs
+            rhs = jnp.where(row == kr, arow, rhs - jnp.where(row > kr, lk, 0.0) * arow)
+        for c in range(k + 1, size):
             cb, cr = divmod(c, 8)
-            f = sub(lk[cb], cr)
-            for b in range(cb, count):
-                cols[c][b] = cols[c][b] - lk[b] * f
-    return lower, rhs
+            cols[c] = cols[c] - lk * sub(lower[k][cb], cr)
+    solved.append(rhs)
 
 
 def krylov(
     mesh_sizes, nb, nr, ly, lz,
     rhs_hbm, blk_hbm, q_ref, p3, small,
-    rv, bv, cf, cz, vp, p1, p2, xb, xg, zs, zr, zp, hz, loc, aa, rbc,
+    rv, bv, cf, cz, vp, p1, p2, xb, xg, zs, zr, zp, hz, loc, aa, rbc, xr, xa,
     x_send, x_recv, y_send, y_recv, z_send, z_recv, a_send, a_recv, in_sem, known,
 ):
     nx, ny, nz = mesh_sizes
@@ -223,7 +225,7 @@
         for a in range(nb):
             vp[0, 1 + y, a * 8:(a + 1) * 8] = rv[pl.ds(a * nr * ly + y, 8, stride=ly), :]
     near_wait(barrier, AXES)
-    for y in order:
+    for y in order[:2]:
         send_x(0, y)
     if waves:
         near(known.at[0], wave_axes)
@@ -262,9 +264,35 @@
     trace = jnp.zeros((ly, 128), F32)
     for i in range(nb):
         trace = trace + cf[0, i, i * ly:(i + 1) * ly]
-
-    def pairs(body, acc):
-        return lax.fori_loop(0, nb // 2, lambda t, acc: body(2 * t + 1, body(2 * t, acc)), acc)
+    lane_sum = lambda x: jnp.sum(x, axis=1, keepdims=True)
+    traces = lane_sum(jnp.sum(trace, axis=0, keepdims=True))
+    sizes = lane_sum(jnp.sum(total_abs, axis=0, keepdims=True))
+    totals = jnp.where(lane[0:1] == 0, traces, jnp.where(lane[0:1] == 1, sizes, 0.0))
+
+    def cross(buf, m, part):
+        buf[gx] = part
+        for d in range(1, nx):
+            remote(buf.at[gx], buf.at[gx], a_send.at[min(m, 1)], a_recv.at[4 + m],
+                   {"gx": wrapped(gx, d, nx)}).start()
+
+    def crossed(buf, m):
+        if nx > 1:
+            take(buf.at[0:nx - 1], a_recv.at[4 + m])
+        return jnp.sum(buf[...], axis=0)
+
+    if nx <= 2:
+        cross(xa, 0, totals)
+    for y in order[2:]:
+        send_x(0, y)
+
+    def several(count, body, acc):
+        def steps(t, acc):
+            for u in range(count):
+                acc = body(count * t + u, acc)
+            return acc
+        return lax.fori_loop(0, nb // count, steps, acc)
+
+    pairs = functools.partial(several, 2)
 
     views = [(vp, (0,), 1), (p1, (), 0), (p2, (), 1), (p3, (), 0)]
     raw = [(vp, (0,), 1), (vp, (1,), 1)]
@@ -284,7 +312,7 @@
             p = tile(n, y, a, own)
             return tuple(acc[i * 8 + s] + p * tile_row(i, y, a * 8 + s, own)
                          for i in range(n + 1) for s in range(8))
-        return pairs(body, acc)
+        return several(4, body, acc)
 
     def gram_zero(n):
         return tuple(empty() for _ in range(8 * (n + 1)))
@@ -315,31 +343,36 @@
     def ends(at, size):
         return [jnp.where(2 * at < size, size - 1 - k, k) for k in range(size)]
 
-    def ar_start(buf, m, rows):
+    def ar_start(buf, m, rows, plane=False):
+        mine = gy * nz + gz if plane else me
         for r, v in enumerate(rows):
-            buf[me, r:r + 1] = v
+            buf[mine, r:r + 1] = v
+
+        def to(device):
+            return remote(buf.at[mine], buf.at[mine], a_send.at[min(m, 1)], a_recv.at[m], device)
+
         if ndev <= 64:
             xs = [wrapped(gx, nx - 1 - d, nx) for d in range(nx)]
             ys = [wrapped(gy, (d + ny // 2) % ny, ny) for d in range(ny)]
             for z in ends(gz, nz):
-                for dx in range(nx):
+                for dx in range(nx - 1 if plane else 0, nx):
                     for dy in range(ny):
-                        copy = remote(buf.at[me], buf.at[me], a_send.at[min(m, 1)], a_recv.at[m], (xs[dx], ys[dy], z))
                         own = dx == nx - 1 and (dy + ny // 2) % ny == 0
-                        when(z != gz if own else None, copy.start)
+                        when(z != gz if own else None, to((xs[dx], ys[dy], z)).start)
         else:
+            count = ny * nz if plane else ndev
+
             def body(d, c):
-                t = lax.rem(me + d, ndev)
-                remote(buf.at[me], buf.at[me], a_send.at[min(m, 1)], a_recv.at[m],
-                       (t // (ny * nz), (t // nz) % ny, t % nz)).start()
+                t = lax.rem(mine + d, count)
+                to((gx if plane else t // (ny * nz), (t // nz) % ny, t % nz)).start()
                 return c
-            lax.fori_loop(1, ndev, body, 0)
-
-    def ar_done(buf, m):
-        take(buf.at[0:ndev - 1], a_recv.at[m])
-        return jnp.sum(buf[...], axis=0)
-
-    lane_sum = lambda x: jnp.sum(x, axis=1, keepdims=True)
+            lax.fori_loop(1, count, body, 0)
+
+    def ar_done(buf, m, count=ndev):
+        take(buf.at[0:count - 1], a_recv.at[m])
+        return jnp.sum(buf[0:count], axis=0)
+
+    sum_r, sum_b, sum_c = (rbc.at[k * ndev:(k + 1) * ndev] for k in range(3))
 
     def own_row(field, y):
         def body(j, acc):
@@ -354,18 +387,19 @@
                 for i in range(nb):
                     acc[i] = acc[i] + spread(cf, (k, i), j * ly + y) * v
             return tuple(acc)
-        acc = pairs(body, tuple(empty() for _ in range(nb)))
+        acc = several(4, body, tuple(empty() for _ in range(nb)))
         for i in range(nb):
             loc[y, i * 8:(i + 1) * 8] = acc[i]
 
-    def edge_row(n, y, plus, minus, field):
+    def edge_cells(y, plus, minus):
         for j in range(nb):
             first = pltpu.roll(minus, lz - 2 * j, 1) if j else minus
-            hz[j * 8:(j + 1) * 8] = jnp.where(lane == 0, first, pltpu.roll(plus, lz - 2 - 2 * j, 1))
-
+            hz[y, j * 8:(j + 1) * 8] = jnp.where(lane == 0, first, pltpu.roll(plus, lz - 2 - 2 * j, 1))
+
+    def edge_row(y, field):
         def body(j, acc):
             at = pl.ds(pl.multiple_of(j * 8, 8), 8)
-            values = [(cz, (), hz[at, :])]
+            values = [(cz, (), hz[y, at, :])]
             if y == ly - 1:
                 values.append((cf, (3,), field(ly, at)))
             if y == 0:
@@ -413,27 +447,23 @@
         own_row(rows_of(vp.at[0]), y)
     if waves:
         near_wait(known.at[(waves - 1) % 2], wave_axes)
+    if nx > 2:
+        cross(xa, 0, totals)
     greet(known.at[2], "gy")
     h00 = gram_end(gram(0), 16)
-    traces = lane_sum(jnp.sum(trace, axis=0, keepdims=True))
-    sizes = lane_sum(jnp.sum(total_abs, axis=0, keepdims=True))
-    totals = jnp.where(lane[0:1] == 0, traces, jnp.where(lane[0:1] == 1, sizes, 0.0))
-
-    def presence(step):
-        if step == min(1, ly - 1):
-            pl.semaphore_wait(known.at[2], ny - 1)
-            greet(known.at[3], "gx")
-        if step == ly - 1:
-            pl.semaphore_wait(known.at[3], nx - 1)
-            ar_start(aa, 0, [totals])
+    def start_totals():
+        pl.semaphore_wait(known.at[2], ny - 1)
+        greet(known.at[3], "gx")
+        ar_start(aa, 0, [crossed(xa, 0)], plane=True)
 
     for n in range(ITERS - 1):
         for step, y in enumerate(order):
-            if n == 0:
-                presence(step)
+            if n == 0 and step == min(2, ly - 1):
+                start_totals()
             z_arrived(n, y)
             y_arrived(n, y)
-            edge_row(n, y, zr[n, y, 0], zr[n, y, 1], rows_of(vp.at[n]))
+            edge_cells(y, zr[n, y, 0], zr[n, y, 1])
+            edge_row(y, rows_of(vp.at[n]))
             acc = x_terms(n, y, lambda side, y, at: xb[n, side, y, at, :])
             for i in range(nb):
                 vp[n + 1, 1 + y, i * 8:(i + 1) * 8] = acc[i]
@@ -445,9 +475,9 @@
         if n + 1 < ITERS - 1:
             for y in order:
                 own_row(rows_of(vp.at[n + 1]), y)
-            ar_start(rbc.at[0], 1, pack32(gram_end(gram(1)) + h00))
-
-    sums = ar_done(aa, 0)
+            cross(xr, 1, jnp.concatenate(pack32(gram_end(gram(1)) + h00), axis=0))
+
+    sums = ar_done(aa, 0, ny * nz)
     sig1 = jnp.broadcast_to(sums[:, 0:1] / (8.0 * cells), (1, 128))
     nu1 = jnp.broadcast_to(sums[:, 1:2] / (8.0 * cells), (1, 128))
     inv1 = 1.0 / nu1
@@ -459,7 +489,10 @@
         for j in range(nb):
             shifted(j, y, p2[1 + y, j * 8:(j + 1) * 8])
     g2 = gram_end(gram(2))
-    ar_start(rbc.at[1], 2, pack32(g2))
+    pl.semaphore_wait(known.at[3], nx - 1)
+    ar_start(sum_b, 2, pack32(g2))
+    pair = crossed(xr, 1)
+    ar_start(sum_r, 1, [pair[0:1], pair[1:2]], plane=True)
 
     for side in range(len(x_sides)):
         for y in range(ly):
@@ -467,18 +500,23 @@
     for y in order:
         own_row(rows_of(p2), y)
     acc3 = gram_zero(3)
-    for y in order:
-        z_arrived(2, y)
-        y_arrived(2, y)
-        for h, near in ((0, 0), (ly + 1, ly - 1)):
-            if y == near:
-                p2[h] = shift2(vp[0, h], vp[1, h], vp[2, h])
-        edge_row(2, y, *(shift2(zr[0, y, s], zr[1, y, s], zr[2, y, s]) for s in range(2)), rows_of(p2))
-        acc = x_terms(2, y, lambda side, y, at: (xb[2, side, y, at, :] * inv1 - xg[side, y, at, :]) * inv1)
-        for i in range(nb):
-            p3[y, i * 8:(i + 1) * 8] = (acc[i] - sig1 * p2[1 + y, i * 8:(i + 1) * 8]) * inv1
-        acc3 = gram_row(3, y, acc3)
-    ar_start(rbc.at[2], 3, pack32(gram_end(acc3)))
+    for group in (order[:-1], order[-1:]):
+        for y in group:
+            z_arrived(2, y)
+            y_arrived(2, y)
+        for y in group:
+            for h, beside in ((0, 0), (ly + 1, ly - 1)):
+                if y == beside:
+                    p2[h] = shift2(vp[0, h], vp[1, h], vp[2, h])
+            edge_cells(y, *(shift2(zr[0, y, s], zr[1, y, s], zr[2, y, s]) for s in range(2)))
+        for y in group:
+            edge_row(y, rows_of(p2))
+        for y in group:
+            acc = x_terms(2, y, lambda side, y, at: (xb[2, side, y, at, :] * inv1 - xg[side, y, at, :]) * inv1)
+            for i in range(nb):
+                p3[y, i * 8:(i + 1) * 8] = (acc[i] - sig1 * p2[1 + y, i * 8:(i + 1) * 8]) * inv1
+            acc3 = gram_row(3, y, acc3)
+    ar_start(sum_c, 3, pack32(gram_end(acc3)))
 
     def emit(n):
         cols = [column(weights[n], c) for c in range(8 * (n + 1))]
@@ -494,26 +532,30 @@
                     parts.append(part)
                 q_ref[n, pl.ds(a * nr * ly + y, 8, stride=ly), :] = sum(parts[1:], parts[0])
 
-    h = unpack32(ar_done(rbc.at[0], 1))
+    h = unpack32(ar_done(sum_r, 1, ny * nz))
     turn = jnp.concatenate([h] + [empty()] * 15, axis=0).T[0:8]
     both = pltpu.roll(h, 8, 1) + pltpu.roll(turn, 8, 1)
     first = pltpu.roll(h, 112, 1)
     g1 = jnp.where(lane < 8, (h - sig1 * first) * inv1,
                    ((h - sig1 * both) + sig1 * sig1 * pltpu.roll(h, 120, 1)) * (inv1 * inv1))
-    grams = [first, g1, unpack32(ar_done(rbc.at[1], 2))]
-    units = [[jnp.where(lane == 8 * n + row, 1.0, 0.0).astype(F32)] for n in range(ITERS)]
-    lower, weights = cholesky([functools.partial(column, g) for g in grams], units, row)
-    weights = [w[0] for w in weights]
+    lower, scale, weights = [], [], []
+
+    def block(n, g):
+        unit = jnp.where(lane == 8 * n + row, 1.0, 0.0).astype(F32)
+        factor_block(functools.partial(column, g), unit, lower, scale, weights, row)
+        emit(n)
+
+    block(0, first)
+    block(1, g1)
+    block(2, unpack32(ar_done(sum_b, 2)))
     factors = [tree([jnp.where(lane == k, lower[k][n], 0.0) for k in range(8 * (n + 1))]) for n in range(ITERS)]
-    for n in range(ITERS):
-        emit(n)
 
     h = dot_nn(jnp.concatenate(weights + [empty()], axis=0), pad_rows(factors[1:]))
     hr = lax.broadcasted_iota(jnp.int32, (32, 128), 0)
     hl = lax.broadcasted_iota(jnp.int32, (32, 128), 1)
     h = h * nu1 + jnp.where(hr == hl, sig1, 0.0)
     turned = jnp.concatenate([h, weights[2] * nu1] + [empty()] * 11, axis=0).T
-    small[8:32] = jnp.concatenate(weights + [empty()] * 13, axis=0).T[0:24]
+    small[8:32] = jnp.concatenate(weights, axis=0)
     small[32:40] = pltpu.roll(turned[16:24], 96, 1)
     for i in range(ITERS + 1):
         for j in range(ITERS):
@@ -525,9 +567,9 @@
     for to, both_sides, one_side, sem in ((z_to, zr, zs, z_send), (y_to, vp.at[:, 0:2], vp.at[:, 0], y_send)):
         pl.when(jnp.logical_and(to[0], to[1]))(lambda: take(both_sides, sem.at[0]))
         pl.when(to[0] != to[1])(lambda: take(one_side, sem.at[0]))
-    take(aa.at[0:ndev - 1], a_send.at[0])
-    take(rbc.at[:, 0:ndev - 1], a_send.at[1])
-    small[0:8] = unpack32(ar_done(rbc.at[2], 3))
+    take(aa.at[0:ny * nz - 1 + nx - 1], a_send.at[0])
+    take(rbc.at[0:2 * (ndev - 1) + ny * nz - 1 + nx - 1], a_send.at[1])
+    small[0:8] = unpack32(ar_done(sum_c, 3))
 
 
 def finish(nb, nr, ly, q_ref, p3, small, basis_hbm, hess_hbm, rest, ob, hs, sem):
@@ -536,8 +578,9 @@
         pltpu.make_async_copy(q_ref.at[n], basis_hbm.at[n], sem.at[0]).start()
     base = 8 * ITERS
     d = small[0:8]
-    dcols = [column(d, c) for c in range(base + 8)]
-    rt = tree([dcols[c] * spread(small, (), 8 + c) for c in range(base)])
+    d = jnp.where(lane < base + 8, d, 0.0)
+    rt = dot_nt(d, pad_rows([small[8 * (n + 1):8 * (n + 2)] for n in range(ITERS)]))
+    s = pltpu.roll(d, 128 - base, 1) - dot_nt(rt, pad_rows([rt]))
     cols = [column(rt, c) for c in range(base)]
     w2 = small[32:40]
 
@@ -561,14 +604,12 @@
             parts = [cols[8 * i + t] * spread(q_ref, (i,), a * nr * ly + t * ly + y) for i in range(ITERS) for t in range(8)]
             rest[y, a * 8:(a + 1) * 8] = p3[y, a * 8:(a + 1) * 8] - tree(parts)
 
-    def gram_column(c):
-        return dcols[base + c] - tree([cols[m] * sub(cols[m], c) for m in range(base)])
-
     unit = jnp.where(lane == row, 1.0, 0.0).astype(F32)
-    lower, inverse = cholesky([gram_column], [[unit]], row)
+    lower, inverse = [], []
+    factor_block(functools.partial(column, s), unit, lower, [], inverse, row)
     last(ITERS, [lk[0] for lk in lower])
     pltpu.make_async_copy(hs, hess_hbm, sem.at[1]).start()
-    cols = [column(inverse[0][0], c) for c in range(8)]
+    cols = [column(inverse[0], c) for c in range(8)]
     half = nb // 2
     for h in range(2):
         for a in range(h * half, (h + 1) * half):
@@ -615,13 +656,13 @@
             vm(ITERS, ly, 8, lz),
             vm(ITERS, ly, 2, 8, lz),
             vm(ly, 2, nb * 8, lz),
-            vm(nb * 8, lz),
             vm(ly, nb * 8, lz),
-            vm(ndev, 1, lz), vm(3, ndev, 2, lz),
+            vm(ly, nb * 8, lz),
+            vm(ndev, 1, lz), vm(3 * ndev, 2, lz), vm(nx, 2, lz), vm(nx, 1, lz),
             dma((sides,)), dma((2, sides, ly)),
             dma((1,)), dma((2, 2)),
             dma((1,)), dma((2, ly)),
-            dma((2,)), dma((4,)),
+            dma((2,)), dma((6,)),
             dma((2,)),
             pltpu.SemaphoreType.REGULAR((4,)),
         ],

time: 23.6 us -> 23.5 us (level)
  no operation moved by 1% of the time
where the time goes in v4:
time: 23.5 us; the launch traced here: 23.4 us
  Pallas kernels  22.7 us (97%)
  between operations  0.64 us (3%)
    pallas_call x1, Pallas kernels, shards(): pl.pallas_call(functools.partial(krylov, mesh_sizes, nb, nr, ly, lz), out...  21.4 us
    pallas_call x1, Pallas kernels, shards(): pl.pallas_call(functools.partial(finish, nb, nr, ly), out_shape=(jax.Shap...  1.35 us

profile of v4, /device:TPU:0, one launch (start us, length us, event | category | flops | bytes accessed | tf_op | source)
XLA Modules:
  0.0 23.4 jit_solution(17276073777823074576)
XLA Ops:
  0.6 21.4 %shard_map.41 = (f32[3,256,128]{2,1,0:T(8,128)S(1)}, f32[4,64,128]{2,1,0:T(8,128)S(1)}, f32[136,128]{1,0:T(8,128)S(1)}) custom-call(f32[256,128]{1,0:T(8,128)} %bitcast.7, bf16[7,8,32,128]{3,2,1,0:T(8,128)(2,1)} %bitcast.6), custom_call_target="tpu_custom_call" | custom-call | tf_op jit(solution)/shard_map/pallas_call | solution.py:637
  22.0 1.3 %shard_map.42 = (f32[4,256,128]{2,1,0:T(8,128)}, f32[4,3,8,8]{3,2,1,0:T(8,128)}) custom-call(f32[3,256,128]{2,1,0:T(8,128)S(1)} %get-tuple-element.7.q_ref, f32[4,64,128]{2,1,0:T(8,128)S(1)} %get-tuple-element.8.p3, f32[136,128]{1,0:T(8,128)S(1)} %get-tuple-element.9.small), custom_call_target="tpu_custom_call" | custom-call | tf_op jit(solution)/shard_map/pallas_call | solution.py:671

commit v5 on v4

--- a/solution.py
+++ b/solution.py
@@ -500,7 +500,7 @@
     for y in order:
         own_row(rows_of(p2), y)
     acc3 = gram_zero(3)
-    for group in (order[:-1], order[-1:]):
+    for group in (order[:-2], order[-2:-1], order[-1:]):
         for y in group:
             z_arrived(2, y)
             y_arrived(2, y)

time: 23.5 us -> 23.5 us (level)
  no operation moved by 1% of the time
where the time goes in v5:
time: 23.5 us; the launch traced here: 23.4 us
  Pallas kernels  22.7 us (97%)
  between operations  0.64 us (3%)
    pallas_call x1, Pallas kernels, shards(): pl.pallas_call(functools.partial(krylov, mesh_sizes, nb, nr, ly, lz), out...  21.4 us
    pallas_call x1, Pallas kernels, shards(): pl.pallas_call(functools.partial(finish, nb, nr, ly), out_shape=(jax.Shap...  1.35 us

profile of v5, /device:TPU:0, one launch (start us, length us, event | category | flops | bytes accessed | tf_op | source)
XLA Modules:
  0.0 23.4 jit_solution(215034583333170253)
XLA Ops:
  0.6 21.4 %shard_map.41 = (f32[3,256,128]{2,1,0:T(8,128)S(1)}, f32[4,64,128]{2,1,0:T(8,128)S(1)}, f32[136,128]{1,0:T(8,128)S(1)}) custom-call(f32[256,128]{1,0:T(8,128)} %bitcast.7, bf16[7,8,32,128]{3,2,1,0:T(8,128)(2,1)} %bitcast.6), custom_call_target="tpu_custom_call" | custom-call | tf_op jit(solution)/shard_map/pallas_call | solution.py:637
  22.0 1.3 %shard_map.42 = (f32[4,256,128]{2,1,0:T(8,128)}, f32[4,3,8,8]{3,2,1,0:T(8,128)}) custom-call(f32[3,256,128]{2,1,0:T(8,128)S(1)} %get-tuple-element.7.q_ref, f32[4,64,128]{2,1,0:T(8,128)S(1)} %get-tuple-element.8.p3, f32[136,128]{1,0:T(8,128)S(1)} %get-tuple-element.9.small), custom_call_target="tpu_custom_call" | custom-call | tf_op jit(solution)/shard_map/pallas_call | solution.py:671
